TPU v7x, 32 devices: a whole 2x2x4 slice. The times are simulated.
32 devices in a mesh: tile: 2 (over y), wave: 16 (over z, x, core).
Axes of the slice: x: 2, y: 2, z: 4, core: 2. Of those that a mesh axis runs over, the one named last changes fastest.
Arguments:
- frames: float32 [4, 1024, 4096], P(None, ('tile', 'wave')), parts along dimension 1, may hold values from -6 to 6
- inverse_var: float32 [4, 1024, 4096], P(None, ('tile', 'wave')), parts along dimension 1, may hold values from 0.2 to 240
- masked: int32 [4, 1024, 4096], P(None, ('tile', 'wave')), parts along dimension 1, may hold values 0 or 1
- psf_band: float32 [4, 1024, 16], P(None, ('tile', 'wave')), parts along dimension 1, may hold values from 0.02 to 0.2
- offsets: int32 [32], P(('tile', 'wave')), parts along dimension 0, may hold values from 18 to 31
- starts: int32 [32, 500], P(('tile', 'wave')), parts along dimension 0, may hold values from 0 to 3995, as said below
- profile: float32 [32, 12, 500], P(('tile', 'wave')), parts along dimension 0, may hold values from 0.05 to 0.5
- flux_start: float32 [1024, 500], P(('tile', 'wave')), parts along dimension 0, may hold values from -3 to 3
Outputs:
- solution: float32 [1024, 500], P(('tile', 'wave')), parts along dimension 0
- residual: float32 [1024, 500], P(('tile', 'wave')), parts along dimension 0
There are 2 independent parts, one for each index of `tile`. A program takes and returns all parts, laid end to end along the dimension named above; each array names one. Nothing has to cross between parts.
Inputs may be any that keep to these rules, and one draw needn't show every extreme that they name: In every slab, fiber k's trace starts at a column from 8k to 8k + 3, so the fibers lie in order, 8 columns apart give or take 3, and neighbouring profiles intersect.
All inputs are finite; a program needn't handle non-finite values. No bound on the sum of `masked` on one device may be relied on, other than what follows from the above.
Results may differ from a plain program's by a relative error of at most 0.0003.
Values sent between devices are 32-bit elements; how exact they have to be, the bound alone decides.
No kernel may reach another device: no remote copies, remote signals or barrier semaphores. Data moves between devices by JAX's collectives and lax.ppermute only.
A program may use at most 64 MiB of HBM per device.

v0:
```python
import functools

import jax
import jax.numpy as jnp
from jax import lax
from jax.experimental import pallas as pl
from jax.experimental.pallas import tpu as pltpu
from jax.sharding import PartitionSpec as P

SLAB_ROWS = 32
HALO = 32
BAND = 16
PW = 12
PITCH = 8
RIDGE = 0.2
GHOST = 16
EXT = SLAB_ROWS + 2 * GHOST
HALF = EXT // 2
LANES = 128
FB = 128
CB = FB * PITCH
SHIFT = 10.0
PRECISE = lax.Precision.HIGHEST
F32 = jnp.float32


def dot(a, b):
    return lax.dot_general(a, b, (((1,), (0,)), ((), ())), precision=PRECISE, preferred_element_type=F32)


def pixel_kernel(starts, profile, frames, inverse_var, masked, inv_edge, mask_edge, frames_edge,
                 t0, t1, f, lo_s, hi_s, pad_s, start_s):
    block = pl.program_id(0)
    fib = starts.shape[1]
    width = pad_s.shape[1]

    @pl.when(block == 0)
    def _():
        pad_s[...] = jnp.zeros_like(pad_s)
        pad_s[0:PW, 0:fib] = profile[0]
        start_s[...] = jnp.zeros_like(start_s)
        start_s[0:1, 0:fib] = starts[...]
        lane = lax.broadcasted_iota(jnp.int32, (1, width), 1)
        jitter = start_s[0:1, :] - PITCH * lane
        base = pad_s[...]
        local = jnp.where(jitter == 0, base, 0.0)
        for d in range(1, 4):
            local = jnp.where(jitter == d, pltpu.roll(base, d, 0), local)
        low, high = local[0:8], local[8:16]
        nxt = pltpu.roll(low, width - 1, 1)
        lo_s[0] = low
        hi_s[0] = high
        lo_s[1] = low * low
        hi_s[1] = high * high
        lo_s[2] = jnp.zeros_like(low)
        hi_s[2] = high * nxt

    cols = pl.ds(pl.multiple_of(block * FB, FB), FB)
    q = lax.broadcasted_iota(jnp.int32, (FB, 8, FB), 0)
    k = lax.broadcasted_iota(jnp.int32, (FB, 8, FB), 2)
    on, after = q == k, q == k + 1
    edge_row = lax.broadcasted_iota(jnp.int32, (FB, FB), 0)
    edge_lane = lax.broadcasted_iota(jnp.int32, (FB, FB), 1)
    edge_on = (edge_row < 8) & (edge_lane == FB - 1)

    def expand(i):
        low = lo_s[i, :, cols][None]
        high = hi_s[i, :, cols][None]
        main = jnp.where(on, low, jnp.where(after, high, 0.0)).reshape(FB * 8, FB)
        tail = jnp.where(edge_on, jnp.concatenate([hi_s[i, :, cols], jnp.zeros((FB - 8, FB), F32)], 0), 0.0)
        return main, tail

    rows = t0.shape[0]
    weight = (inverse_var[...] * (1.0 - masked[...].astype(F32))).reshape(rows, CB)
    weight_e = (inv_edge[...] * (1.0 - mask_edge[...].astype(F32))).reshape(rows, FB)
    data = weight * frames[...].reshape(rows, CB)
    data_e = weight_e * frames_edge[...].reshape(rows, FB)
    m, e = expand(1)
    t0[...] = dot(weight, m) + dot(weight_e, e)
    m, e = expand(2)
    t1[...] = dot(weight, m) + dot(weight_e, e)
    m, e = expand(0)
    f[...] = dot(data, m) + dot(data_e, e)


def tri(t0, t1, u):
    width = u.shape[1]
    return t0 * u + t1 * pltpu.roll(u, width - 1, 1) + pltpu.roll(t1 * u, 1, 1)


def split(ext, parity, send_e, send_o, at):
    low, high = ext[0:HALF], ext[HALF:EXT]
    send_e[at : at + HALF, :] = jnp.where(parity == 0, high, low)
    send_o[at : at + HALF, :] = jnp.where(parity == 0, low, high)


def joined(part, got_e, got_o, parity, at):
    e, o = got_e[at : at + HALF, :], got_o[at : at + HALF, :]
    low = jnp.where(parity == 0, o, e)
    high = jnp.where(parity == 0, e, o)
    return jnp.concatenate([part[0:HALF, :] + low, part[HALF:EXT, :] + high], 0)


def lanes_of(x):
    s = jnp.sum(x, axis=0, keepdims=True)
    total = s[:, 0:LANES]
    for i in range(1, x.shape[1] // LANES):
        total = total + s[:, i * LANES : (i + 1) * LANES]
    return total


def own(x):
    return x[GHOST : GHOST + SLAB_ROWS, :]


def first_kernel(info, band, flux, flux_e, flux_o, t0, t1, f, rowmat, rowmat_t, start_ext, part, send_e, send_o, ext_s, band_s):
    parity, offset, is_first, is_last = info[0], info[1], info[2], info[3]
    fib = flux.shape[1]
    rows = t0.shape[0]
    ext_s[...] = jnp.zeros_like(ext_s)
    e, o = flux_e[...], flux_o[...]
    ext_s[0:GHOST, 0:fib] = jnp.where(parity == 0, o, e)
    ext_s[GHOST : GHOST + SLAB_ROWS, 0:fib] = flux[...]
    ext_s[GHOST + SLAB_ROWS : EXT, 0:fib] = jnp.where(parity == 0, e, o)
    band_s[...] = jnp.zeros_like(band_s)
    band_s[:, 0:BAND] = band[...].reshape(rows, BAND)
    r = band_s[...]
    place = lax.rem(lax.broadcasted_iota(jnp.int32, r.shape, 0), SLAB_ROWS)
    bit = 1
    while bit < SLAB_ROWS:
        r = jnp.where((place & bit) != 0, pltpu.roll(r, bit, 1), r)
        bit *= 2
    r = pltpu.roll(r, offset - (HALO - GHOST), 1)
    lane = lax.broadcasted_iota(jnp.int32, r.shape, 1)
    outside = ((is_first == 1) & (lane < GHOST)) | ((is_last == 1) & (lane >= GHOST + SLAB_ROWS))
    r = jnp.where(outside, 0.0, r)
    rt = r.T[0:EXT, :]
    r = r[:, 0:EXT]
    rowmat[...] = r
    rowmat_t[...] = rt
    ext = ext_s[...]
    start_ext[...] = ext
    t = f[...] - tri(t0[...], t1[...], dot(r, ext))
    back = dot(rt, t)
    diag = dot(rt * rt, t0[...])
    part[0:EXT, :] = back
    part[EXT : 2 * EXT, :] = diag
    split(back, parity, send_e, send_o, 0)
    split(diag, parity, send_e, send_o, HALF)


def apply_rows(vec, rowmat, rowmat_t, t0, t1):
    u = dot(rowmat[...], vec)
    t = tri(t0[...], t1[...], u)
    return u, t, dot(rowmat_t[...], t)


def second_kernel(info, rowmat, rowmat_t, t0, t1, start_ext, part, got_e, got_o, diag, vec, mom, part_out, send_e, send_o):
    parity = info[0]
    res = joined(part[0:EXT, :], got_e, got_o, parity, 0) - RIDGE * start_ext[...]
    d = joined(part[EXT : 2 * EXT, :], got_e, got_o, parity, HALF) + RIDGE
    p = res / d
    diag[...] = d
    vec[...] = p
    mom[...] = jnp.zeros_like(mom)
    mom[0:1, :] = lanes_of(own(p) * own(res))
    _, _, back = apply_rows(p, rowmat, rowmat_t, t0, t1)
    part_out[...] = back
    split(back, parity, send_e, send_o, 0)


def next_kernel(step, copies, info, rowmat, rowmat_t, t0, t1, diag, before, mom, part, got_e, got_o, vec, mom_out, part_out, send_e, send_o):
    parity = info[0]
    prev = before[...]
    d = diag[...]
    image = joined(part, got_e, got_o, parity, 0) + RIDGE * prev
    p = image / d - SHIFT * prev
    vec[...] = p
    scaled = own(d) * own(p)
    u, t, back = apply_rows(p, rowmat, rowmat_t, t0, t1)
    part_out[...] = back
    split(back, parity, send_e, send_o, 0)
    moments = mom[...]
    row = lax.broadcasted_iota(jnp.int32, moments.shape, 0)
    new = [(2 * step - 1, lanes_of(scaled * own(prev))), (2 * step, lanes_of(scaled * own(p)))]
    if copies:
        new.append((2 * step + 1, lanes_of(u * t) + RIDGE * lanes_of(own(p) * own(p))))
    for i, value in new:
        moments = jnp.where(row == i, value, moments)
    if copies:
        mom_out[...] = jnp.broadcast_to(moments[None], mom_out.shape)
    else:
        mom_out[...] = moments


def coefficients(mom):
    mu = [mom[i : i + 1, :] for i in range(5)]
    nu = [mu[i + 1] + SHIFT * mu[i] for i in range(4)] + [mom[5:6, :]]

    def inner(p, w):
        total = None
        for i in range(len(p)):
            for j in range(len(p)):
                term = p[i] * p[j] * w[i + j]
                total = term if total is None else total + term
        return total

    one = jnp.ones_like(mu[0])
    rho, delta, energy = [one], [one], mu[0]
    chi = []
    for step in range(3):
        alpha = energy / inner(delta, nu)
        chi = [c + alpha * x for c, x in zip(chi + [0.0 * one], delta)]
        image = [SHIFT * x for x in delta] + [0.0 * one]
        image = [x + (delta[i - 1] if i else 0.0) for i, x in enumerate(image)]
        rho = [x - alpha * y for x, y in zip(rho + [0.0 * one], image)]
        if step < 2:
            fresh = inner(rho, mu)
            beta = fresh / energy
            delta = [x + beta * y for x, y in zip(rho, delta + [0.0 * one])]
            energy = fresh
    return chi, rho


def last_kernel(info, moms, diag, start_ext, p0, p1, p2, part, got_e, got_o, solution_ref, residual_ref):
    parity = info[0]
    fib = solution_ref.shape[1]
    total = jnp.sum(moms[...], axis=0)
    total = jnp.broadcast_to(jnp.sum(total, axis=1, keepdims=True), total.shape)
    chi, rho = coefficients(total)
    width = diag.shape[1]

    def wide(c):
        return jnp.concatenate([c] * (width // LANES), 1)

    chi = [wide(c) for c in chi]
    rho = [wide(c) for c in rho]
    q0, q1, q2, d = own(p0), own(p1), own(p2), own(diag)
    image = own(joined(part, got_e, got_o, parity, 0)) + RIDGE * q2
    x = own(start_ext) + chi[0] * q0 + chi[1] * q1 + chi[2] * q2
    r = d * (rho[0] * q0 + rho[1] * q1 + rho[2] * q2) + rho[3] * (image - SHIFT * (d * q2))
    solution_ref[...] = x[:, 0:fib]
    residual_ref[...] = r[:, 0:fib]


def swap(values, pairs):
    return lax.ppermute(values, "wave", pairs)


def local(frames, inverse_var, masked, psf_band, offsets, starts, profile, flux_start):
    waves = lax.axis_size("wave")
    fib = flux_start.shape[1]
    expo, slab, columns = frames.shape
    rows = expo * slab
    blocks = columns // CB
    width = blocks * FB
    index = lax.axis_index("wave")
    parity = lax.rem(index, 2)
    even = [(i, i ^ 1) for i in range(waves) if (i ^ 1) < waves]
    odd = [(i, j) for i in range(waves) for j in (((i + 1) ^ 1) - 1,) if 0 <= j < waves and j != i]
    info = jnp.stack([parity, offsets[0], (index == 0).astype(jnp.int32), (index == waves - 1).astype(jnp.int32)])

    first, last = flux_start[0:GHOST], flux_start[SLAB_ROWS - GHOST :]
    flux_o = swap(jnp.where(parity == 0, first, last), odd)
    flux_e = swap(jnp.where(parity == 0, last, first), even)

    vm = pl.BlockSpec(memory_space=pltpu.VMEM)
    sm = pl.BlockSpec(memory_space=pltpu.SMEM)

    def shape(*dims):
        return jax.ShapeDtypeStruct(dims, F32)

    main = pl.BlockSpec((expo, slab, CB), lambda b: (0, 0, b))
    edge = pl.BlockSpec((expo, slab, FB), lambda b: (0, 0, jnp.minimum((b + 1) * (CB // FB), columns // FB - 1)))
    whole2 = pl.BlockSpec((1, fib), lambda b: (0, 0))
    whole3 = pl.BlockSpec((1, PW, fib), lambda b: (0, 0, 0))
    out = pl.BlockSpec((rows, FB), lambda b: (0, b))
    t0, t1, f = pl.pallas_call(
        pixel_kernel,
        grid=(blocks,),
        in_specs=[whole2, whole3, main, main, main, edge, edge, edge],
        out_specs=[out, out, out],
        out_shape=[shape(rows, width)] * 3,
        scratch_shapes=[
            pltpu.VMEM((3, 8, width), F32),
            pltpu.VMEM((3, 8, width), F32),
            pltpu.VMEM((16, width), F32),
            pltpu.VMEM((8, width), jnp.int32),
        ],
        compiler_params=pltpu.CompilerParams(dimension_semantics=("arbitrary",)),
        name="pixels",
    )(starts, profile, frames, inverse_var, masked, inverse_var, masked, frames)

    rowmat, rowmat_t, start_ext, part, send_e, send_o = pl.pallas_call(
        first_kernel,
        in_specs=[sm] + [vm] * 7,
        out_specs=[vm] * 6,
        out_shape=[shape(rows, EXT), shape(EXT, rows), shape(EXT, width), shape(2 * EXT, width), shape(EXT, width), shape(EXT, width)],
        scratch_shapes=[pltpu.VMEM((EXT, width), F32), pltpu.VMEM((rows, LANES), F32)],
        name="first",
    )(info, psf_band, flux_start, flux_e, flux_o, t0, t1, f)
    got_o, got_e = swap(send_o, odd), swap(send_e, even)

    diag, p0, mom, part, send_e, send_o = pl.pallas_call(
        second_kernel,
        in_specs=[sm] + [vm] * 8,
        out_specs=[vm] * 6,
        out_shape=[shape(EXT, width), shape(EXT, width), shape(8, LANES), shape(EXT, width), shape(HALF, width), shape(HALF, width)],
        name="second",
    )(info, rowmat, rowmat_t, t0, t1, start_ext, part, got_e, got_o)
    vectors = [p0]
    for step in (1, 2):
        got_o, got_e = swap(send_o, odd), swap(send_e, even)
        copies = waves if step == 2 else 0
        mom_shape = shape(waves, 8, LANES) if copies else shape(8, LANES)
        vec, mom, part, send_e, send_o = pl.pallas_call(
            functools.partial(next_kernel, step, copies),
            in_specs=[sm] + [vm] * 10,
            out_specs=[vm] * 5,
            out_shape=[shape(EXT, width), mom_shape, shape(EXT, width), shape(HALF, width), shape(HALF, width)],
            name=f"next{step}",
        )(info, rowmat, rowmat_t, t0, t1, diag, vectors[-1], mom, part, got_e, got_o)
        vectors.append(vec)
    got_o, got_e = swap(send_o, odd), swap(send_e, even)
    moms = lax.all_to_all(mom, "wave", 0, 0)
    return tuple(
        pl.pallas_call(
            last_kernel,
            in_specs=[sm] + [vm] * 9,
            out_specs=[vm] * 2,
            out_shape=[shape(slab, fib)] * 2,
            name="last",
        )(info, moms, diag, start_ext, *vectors, part, got_e, got_o)
    )


def solution(mesh):
    placed = (
        P(None, ("tile", "wave"), None),
        P(None, ("tile", "wave"), None),
        P(None, ("tile", "wave"), None),
        P(None, ("tile", "wave"), None),
        P(("tile", "wave")),
        P(("tile", "wave"), None),
        P(("tile", "wave"), None, None),
        P(("tile", "wave"), None),
    )
    return jax.shard_map(
        local,
        mesh=mesh,
        in_specs=placed,
        out_specs=(P(("tile", "wave"), None), P(("tile", "wave"), None)),
        check_vma=False,
    )
```

profile of v0, /device:TPU:0, one launch (start us, length us, event | category | flops | bytes accessed | tf_op | source)
XLA Modules:
  0.0 70.6 jit_solution(16722233019030939059)
XLA Ops:
  0.6 0.8 %slice_select_fusion = (f32[16,500]{1,0:T(8,128)S(1)}, f32[16,500]{1,0:T(8,128)S(1)}) fusion(f32[32,500]{1,0:T(8,128)} %flux.1, pred[]{:T(512)S(6)} %eq.12), kind=kLoop, calls=%fused_computation | loop fusion | flops 16000 | bytes 128001 | tf_op jit(solution)/shard_map/jit(_where)/select_n | solution.py:264
  1.4 0.7 collective-permute-start.1
  2.1 4.4 %collective-permute-start = (f32[16,500]{1,0:T(8,128)S(1)}, f32[16,500]{1,0:T(8,128)S(1)}, u32[]{:S(2)}, u32[]{:S(2)}) collective-permute-start(f32[16,500]{1,0:T(8,128)S(1)} %get-tuple-element.53), channel_id=1, source_target_pairs={{0,1},{1,0},{2,3},{3,2},{4,5},{5,4},{6,7},{7,6},{8,9},{9,8},{10,11... | collective-permute-start | bytes 96008 | tf_op jit(solution)/shard_map/ppermute | solution.py:247
  7.1 0.7 pad_add_fusion.info
  7.8 1.4 %copy.10.profile = f32[1,12,500]{2,1,0:T(8,128)} copy(f32[1,12,500]{2,0,1:T(1,128)} %param.14) | data formatting | bytes 48000 | tf_op args[6]
  9.1 1.5 %copy.11.band = f32[4,32,16]{2,1,0:T(8,128)} copy(f32[4,32,16]{1,2,0:T(8,128)} %param.11) | data formatting | bytes 16384 | tf_op args[3]
  10.6 9.3 %pixels.1 = (f32[128,512]{1,0:T(8,128)}, f32[128,512]{1,0:T(8,128)}, f32[128,512]{1,0:T(8,128)}) custom-call(s32[1,500]{1,0:T(1,128)} %starts.1, f32[1,12,500]{2,1,0:T(8,128)} %copy.10.profile, f32[4,32,4096]{2,1,0:T(8,128)} %frames_edge.1, f32[4,32,4096]{2,1,0:T(8,128)} %inv_edge.1, s32[4,32,4096]{2,1,0:T(8,128)} %mask_edge.1, f32[4,32,4096]{2,1,0:T(8,128)} %inv_edge.1, ...), custom_call_target="tpu_custom_call" | custom-call | tf_op jit(solution)/shard_map/pixels/pallas_call | solution.py:278
  20.0 0.6 copy-done.9
  20.5 0.0 copy-done.10
  20.6 3.3 %first.1 = (f32[128,64]{1,0:T(8,128)}, f32[64,128]{1,0:T(8,128)}, f32[64,512]{1,0:T(8,128)}, f32[128,512]{1,0:T(8,128)}, f32[64,512]{1,0:T(8,128)}, /*index=5*/f32[64,512]{1,0:T(8,128)}) custom-call(s32[4]{0:T(128)} %pad_add_fusion.info, f32[4,32,16]{2,1,0:T(8,128)} %copy.11.band, f32[32,500]{1,0:T(8,128)} %flux.1, f32[16,500]{1,0:T(8,128)} %copy-done.10, ...), custom_call_target="tpu_custom_call" | custom-call | tf_op jit(solution)/shard_map/first/pallas_call | solution.py:294
  23.9 0.7 collective-permute-start.3
  24.6 0.9 %collective-permute-done.2.got_e = f32[64,512]{1,0:T(8,128)S(1)} collective-permute-done((f32[64,512]{1,0:T(8,128)}, f32[64,512]{1,0:T(8,128)S(1)}, u32[]{:S(2)}, u32[]{:S(2)}) %collective-permute-start.2) | collective-permute-done | bytes 131104 | tf_op jit(solution)/shard_map/ppermute | solution.py:247
  25.4 0.6 copy-done.1
  26.1 0.1 copy-done.2
  26.2 2.8 %second.1 = (f32[64,512]{1,0:T(8,128)}, f32[64,512]{1,0:T(8,128)}, f32[8,128]{1,0:T(8,128)}, f32[64,512]{1,0:T(8,128)}, f32[32,512]{1,0:T(8,128)}, /*index=5*/f32[32,512]{1,0:T(8,128)}) custom-call(s32[4]{0:T(128)} %pad_add_fusion.info, f32[128,64]{1,0:T(8,128)} %get-tuple-element.30.rowmat, f32[64,128]{1,0:T(8,128)} %get-tuple-element.31.rowmat_t, ...), custom_call_target="tpu_custom_call" | custom-call | tf_op jit(solution)/shard_map/second/pallas_call | solution.py:304
  28.9 5.4 %collective-permute-start.4 = (f32[32,512]{1,0:T(8,128)}, f32[32,512]{1,0:T(8,128)S(1)}, u32[]{:S(2)}, u32[]{:S(2)}) collective-permute-start(f32[32,512]{1,0:T(8,128)} %get-tuple-element.40), channel_id=1, source_target_pairs={{0,1},{1,0},{2,3},{3,2},{4,5},{5,4},{6,7},{7,6},{8,9},{9,8},{10,11... | collective-permute-start | bytes 196616 | tf_op jit(solution)/shard_map/ppermute | solution.py:247
  34.3 0.7 collective-permute-start.5
  35.0 0.5 collective-permute-done.4.got_e
  35.4 0.6 copy-done.7
  36.1 2.8 %next1.1 = (f32[64,512]{1,0:T(8,128)}, f32[8,128]{1,0:T(8,128)}, f32[64,512]{1,0:T(8,128)}, f32[32,512]{1,0:T(8,128)}, f32[32,512]{1,0:T(8,128)}) custom-call(s32[4]{0:T(128)} %pad_add_fusion.info, f32[128,64]{1,0:T(8,128)} %get-tuple-element.30.rowmat, f32[64,128]{1,0:T(8,128)} %get-tuple-element.31.rowmat_t, f32[128,512]{1,0:T(8,128)} %get-tuple-element.27.t0, ...), custom_call_target="tpu_custom_call" | custom-call | tf_op jit(solution)/shard_map/next1/pallas_call | solution.py:316
  38.8 5.5 %collective-permute-start.6 = (f32[32,512]{1,0:T(8,128)}, f32[32,512]{1,0:T(8,128)S(1)}, u32[]{:S(2)}, u32[]{:S(2)}) collective-permute-start(f32[32,512]{1,0:T(8,128)} %get-tuple-element.45), channel_id=1, source_target_pairs={{0,1},{1,0},{2,3},{3,2},{4,5},{5,4},{6,7},{7,6},{8,9},{9,8},{10,11... | collective-permute-start | bytes 196616 | tf_op jit(solution)/shard_map/ppermute | solution.py:247
  44.3 0.7 collective-permute-start.7
  45.0 0.5 collective-permute-done.6.got_e
  45.4 0.6 copy-done.5
  46.1 2.8 %next2.1 = (f32[64,512]{1,0:T(8,128)}, f32[16,8,128]{2,1,0:T(8,128)}, f32[64,512]{1,0:T(8,128)}, f32[32,512]{1,0:T(8,128)}, f32[32,512]{1,0:T(8,128)}) custom-call(s32[4]{0:T(128)} %pad_add_fusion.info, f32[128,64]{1,0:T(8,128)} %get-tuple-element.30.rowmat, f32[64,128]{1,0:T(8,128)} %get-tuple-element.31.rowmat_t, f32[128,512]{1,0:T(8,128)} %get-tuple-element.27.t0, ...), custom_call_target="tpu_custom_call" | custom-call | tf_op jit(solution)/shard_map/next2/pallas_call | solution.py:316
  48.8 12.1 %all-to-all-start = ((f32[16,8,128]{2,1,0:T(8,128)}), f32[16,8,128]{2,1,0:T(8,128)S(1)}, u32[]{:S(2)}, u32[]{:S(2)}) async-start(f32[16,8,128]{2,1,0:T(8,128)} %get-tuple-element.47), calls=%async_computation | async-start | bytes 131072 | tf_op jit(solution)/shard_map/all_to_all | solution.py:325
  60.9 0.4 collective-permute-start.8
  61.4 0.7 collective-permute-start.9
  62.0 0.5 collective-permute-done.8.got_e
  62.5 5.4 %all-to-all-done.moms = f32[16,8,128]{2,1,0:T(8,128)S(1)} async-done(((f32[16,8,128]{2,1,0:T(8,128)}), f32[16,8,128]{2,1,0:T(8,128)S(1)}, u32[]{:S(2)}, u32[]{:S(2)}) %all-to-all-start) | async-done | bytes 65568 | tf_op jit(solution)/shard_map/all_to_all | solution.py:325
  67.9 0.6 copy-done
  68.5 2.1 %last.1 = (f32[32,500]{1,0:T(8,128)}, f32[32,500]{1,0:T(8,128)}) custom-call(s32[4]{0:T(128)} %pad_add_fusion.info, f32[16,8,128]{2,1,0:T(8,128)} %copy-done, f32[64,512]{1,0:T(8,128)} %get-tuple-element.36.diag, f32[64,512]{1,0:T(8,128)} %get-tuple-element.32.start_ext, f32[64,512]{1,0:T(8,128)} %get-tuple-element.37.before.p0, ...), custom_call_target="tpu_custom_call" | custom-call | tf_op jit(solution)/shard_map/last/pallas_call | solution.py:327
  (22 shorter events, 0.1 us)
Async XLA Ops:
  1.4 18.5 %collective-permute-start.1 = (f32[16,500]{1,0:T(8,128)S(1)}, f32[16,500]{1,0:T(8,128)S(1)}, u32[]{:S(2)}, u32[]{:S(2)}) collective-permute-start(f32[16,500]{1,0:T(8,128)S(1)} %get-tuple-element.52), channel_id=1, source_target_pairs={{1,2},{2,1},{3,4},{4,3},{5,6},{6,5},{7,8},{8,7},{9,10},{10,9},{11,... | collective-permute-start | bytes 96008 | tf_op jit(solution)/shard_map/ppermute | solution.py:247
  2.1 17.9 %collective-permute-start = (f32[16,500]{1,0:T(8,128)S(1)}, f32[16,500]{1,0:T(8,128)S(1)}, u32[]{:S(2)}, u32[]{:S(2)}) collective-permute-start(f32[16,500]{1,0:T(8,128)S(1)} %get-tuple-element.53), channel_id=1, source_target_pairs={{0,1},{1,0},{2,3},{3,2},{4,5},{5,4},{6,7},{7,6},{8,9},{9,8},{10,11... | collective-permute-start | bytes 96008 | tf_op jit(solution)/shard_map/ppermute | solution.py:247
  19.9 0.6 copy-start.9
  19.9 0.6 copy-start.10
  23.9 1.6 %collective-permute-start.2 = (f32[64,512]{1,0:T(8,128)}, f32[64,512]{1,0:T(8,128)S(1)}, u32[]{:S(2)}, u32[]{:S(2)}) collective-permute-start(f32[64,512]{1,0:T(8,128)} %get-tuple-element.34), channel_id=1, source_target_pairs={{0,1},{1,0},{2,3},{3,2},{4,5},{5,4},{6,7},{7,6},{8,9},{9,8},{10,11... | collective-permute-start | bytes 393224 | tf_op jit(solution)/shard_map/ppermute | solution.py:247
  23.9 1.5 %collective-permute-start.3 = (f32[64,512]{1,0:T(8,128)}, f32[64,512]{1,0:T(8,128)S(1)}, u32[]{:S(2)}, u32[]{:S(2)}) collective-permute-start(f32[64,512]{1,0:T(8,128)} %get-tuple-element.35), channel_id=1, source_target_pairs={{1,2},{2,1},{3,4},{4,3},{5,6},{6,5},{7,8},{8,7},{9,10},{10,9},{11,... | collective-permute-start | bytes 393224 | tf_op jit(solution)/shard_map/ppermute | solution.py:247
  25.4 0.6 copy-start.1
  25.4 0.7 %copy-start.2 = (f32[64,512]{1,0:T(8,128)}, f32[64,512]{1,0:T(8,128)S(1)}, u32[]{:S(2)}) copy-start(f32[64,512]{1,0:T(8,128)S(1)} %collective-permute-done.3.got_o) | copy-start | bytes 393220
  28.9 6.5 %collective-permute-start.4 = (f32[32,512]{1,0:T(8,128)}, f32[32,512]{1,0:T(8,128)S(1)}, u32[]{:S(2)}, u32[]{:S(2)}) collective-permute-start(f32[32,512]{1,0:T(8,128)} %get-tuple-element.40), channel_id=1, source_target_pairs={{0,1},{1,0},{2,3},{3,2},{4,5},{5,4},{6,7},{7,6},{8,9},{9,8},{10,11... | collective-permute-start | bytes 196616 | tf_op jit(solution)/shard_map/ppermute | solution.py:247
  34.3 1.1 %collective-permute-start.5 = (f32[32,512]{1,0:T(8,128)}, f32[32,512]{1,0:T(8,128)S(1)}, u32[]{:S(2)}, u32[]{:S(2)}) collective-permute-start(f32[32,512]{1,0:T(8,128)} %get-tuple-element.41), channel_id=1, source_target_pairs={{1,2},{2,1},{3,4},{4,3},{5,6},{6,5},{7,8},{8,7},{9,10},{10,9},{11,... | collective-permute-start | bytes 196616 | tf_op jit(solution)/shard_map/ppermute | solution.py:247
  35.4 0.6 copy-start.7
  35.4 0.6 copy-start.8
  38.8 6.6 %collective-permute-start.6 = (f32[32,512]{1,0:T(8,128)}, f32[32,512]{1,0:T(8,128)S(1)}, u32[]{:S(2)}, u32[]{:S(2)}) collective-permute-start(f32[32,512]{1,0:T(8,128)} %get-tuple-element.45), channel_id=1, source_target_pairs={{0,1},{1,0},{2,3},{3,2},{4,5},{5,4},{6,7},{7,6},{8,9},{9,8},{10,11... | collective-permute-start | bytes 196616 | tf_op jit(solution)/shard_map/ppermute | solution.py:247
  44.3 1.1 %collective-permute-start.7 = (f32[32,512]{1,0:T(8,128)}, f32[32,512]{1,0:T(8,128)S(1)}, u32[]{:S(2)}, u32[]{:S(2)}) collective-permute-start(f32[32,512]{1,0:T(8,128)} %get-tuple-element.46), channel_id=1, source_target_pairs={{1,2},{2,1},{3,4},{4,3},{5,6},{6,5},{7,8},{8,7},{9,10},{10,9},{11,... | collective-permute-start | bytes 196616 | tf_op jit(solution)/shard_map/ppermute | solution.py:247
  45.4 0.6 copy-start.5
  45.4 0.6 copy-start.6
  48.8 19.0 %all-to-all-start = ((f32[16,8,128]{2,1,0:T(8,128)}), f32[16,8,128]{2,1,0:T(8,128)S(1)}, u32[]{:S(2)}, u32[]{:S(2)}) async-start(f32[16,8,128]{2,1,0:T(8,128)} %get-tuple-element.47), calls=%async_computation | async-start | bytes 131072 | tf_op jit(solution)/shard_map/all_to_all | solution.py:325
  60.9 1.5 %collective-permute-start.8 = (f32[32,512]{1,0:T(8,128)}, f32[32,512]{1,0:T(8,128)S(1)}, u32[]{:S(2)}, u32[]{:S(2)}) collective-permute-start(f32[32,512]{1,0:T(8,128)} %get-tuple-element.50), channel_id=1, source_target_pairs={{0,1},{1,0},{2,3},{3,2},{4,5},{5,4},{6,7},{7,6},{8,9},{9,8},{10,11... | collective-permute-start | bytes 196616 | tf_op jit(solution)/shard_map/ppermute | solution.py:247
  61.4 1.1 %collective-permute-start.9 = (f32[32,512]{1,0:T(8,128)}, f32[32,512]{1,0:T(8,128)S(1)}, u32[]{:S(2)}, u32[]{:S(2)}) collective-permute-start(f32[32,512]{1,0:T(8,128)} %get-tuple-element.51), channel_id=1, source_target_pairs={{1,2},{2,1},{3,4},{4,3},{5,6},{6,5},{7,8},{8,7},{9,10},{10,9},{11,... | collective-permute-start | bytes 196616 | tf_op jit(solution)/shard_map/ppermute | solution.py:247
  62.5 5.4 %copy-start.3 = (f32[32,512]{1,0:T(8,128)}, f32[32,512]{1,0:T(8,128)S(1)}, u32[]{:S(2)}) copy-start(f32[32,512]{1,0:T(8,128)S(1)} %collective-permute-done.8.got_e) | copy-start | bytes 196612
  62.5 5.4 %copy-start.4 = (f32[32,512]{1,0:T(8,128)}, f32[32,512]{1,0:T(8,128)S(1)}, u32[]{:S(2)}) copy-start(f32[32,512]{1,0:T(8,128)S(1)} %collective-permute-done.9.got_o) | copy-start | bytes 196612
  67.8 0.6 copy-start
where the time goes:
time: 71.2 us; the launch traced here: 70.6 us
  starting transfers between devices  31.1 us (44%)
  Pallas kernels  23 us (32%)
  waiting for transfers between devices  7.61 us (11%)
  local copies, waits for them, and re-layouts  6.04 us (8%)
  other arithmetic  1.44 us (2%)
  between operations  1.38 us (2%)
    ppermute x10, starting transfers between devices, swap(): return lax.ppermute(values, 'wave', pairs)  19 us
    all_to_all x1, starting transfers between devices, local(): moms = lax.all_to_all(mom, 'wave', 0, 0)  12.1 us
    pallas_call x1, Pallas kernels, local(): pl.pallas_call(pixel_kernel, grid=(blocks,), in_specs=[whole2, whole3, ma...  9.32 us
    unnamed x24, local copies, waits for them, and re-layouts  6.04 us
    pallas_call x2, Pallas kernels, local(): pl.pallas_call(functools.partial(next_kernel, step, copies), in_specs=[sm...  5.51 us
    all_to_all x1, waiting for transfers between devices, local(): moms = lax.all_to_all(mom, 'wave', 0, 0)  5.36 us
    pallas_call x1, Pallas kernels, local(): pl.pallas_call(first_kernel, in_specs=[sm] + [vm] * 7, out_specs=[vm] * 6...  3.31 us
    pallas_call x1, Pallas kernels, local(): pl.pallas_call(second_kernel, in_specs=[sm] + [vm] * 8, out_specs=[vm] *...  2.78 us
  transfers between devices with their start and end apart: 11, of which 5 were waited for; matrix products, arithmetic and copies ran while one was open for 5% of the time, Pallas kernels for 13%

commit v1 on v0

v1 whole, which is shorter than its diff:
```python
import functools

import jax
import jax.numpy as jnp
from jax import lax
from jax.experimental import pallas as pl
from jax.experimental.pallas import tpu as pltpu
from jax.sharding import PartitionSpec as P

SLAB_ROWS = 32
HALO = 32
BAND = 16
PW = 12
PITCH = 8
RIDGE = 0.2
GHOST = 16
EXT = SLAB_ROWS + 2 * GHOST
HALF = EXT // 2
LANES = 128
FB = 128
CB = FB * PITCH
VMEM_LIMIT = 16 * 1024 * 1024
SHIFT = 10.0
PRECISE = lax.Precision.HIGHEST
F32 = jnp.float32
BF16 = jnp.bfloat16


def dot(a, b):
    return lax.dot_general(a, b, (((1,), (0,)), ((), ())), precision=PRECISE, preferred_element_type=F32)


def parts(x):
    high = x.astype(BF16)
    rest = x - high.astype(F32)
    mid = rest.astype(BF16)
    return high, mid, (rest - mid.astype(F32)).astype(BF16)


def mm(a, b):
    return lax.dot_general(a, b, (((1,), (0,)), ((), ())), preferred_element_type=F32)


def row_matrix(rt, offset):
    index = lax.axis_index("wave")
    place = lax.rem(lax.broadcasted_iota(jnp.int32, rt.shape, 1), SLAB_ROWS) + (offset - (HALO - GHOST))
    bit = 1
    while bit < EXT:
        rt = jnp.where((place & bit) != 0, pltpu.roll(rt, bit, 0), rt)
        bit *= 2
    level = lax.broadcasted_iota(jnp.int32, rt.shape, 0)
    outside = ((index == 0) & (level < GHOST)) | ((index == lax.axis_size("wave") - 1) & (level >= GHOST + SLAB_ROWS))
    return jnp.where(outside, 0.0, rt)


def pixel_kernel(offsets, starts, profile, band, frames, inverse_var, masked, t0, t1, f, rowmat, rowmat_t,
                 frames_s, inv_s, mask_s, sems, starts_s, profile_s, bands_s, side_sems, pad_s, start_s, where_s, band_s):
    fib = starts.shape[1]
    rows, width = t0.shape
    sides = [
        pltpu.make_async_copy(src, dst, side_sems.at[i])
        for i, (src, dst) in enumerate(((starts, starts_s), (profile, profile_s), (band, bands_s)))
    ]
    for c in sides:
        c.start()
    blocks = width // FB
    copies = []
    for b in range(blocks):
        cols = pl.ds(b * CB, CB)
        copies.append([
            pltpu.make_async_copy(src.at[:, :, cols], dst.at[:, :, cols], sems.at[b, i])
            for i, (src, dst) in enumerate(((inverse_var, inv_s), (masked, mask_s), (frames, frames_s)))
        ])
    for group in copies:
        for c in group:
            c.start()

    pad_s[...] = jnp.zeros_like(pad_s)
    start_s[...] = jnp.zeros_like(start_s)
    band_s[...] = jnp.zeros_like(band_s)
    group = lax.broadcasted_iota(jnp.int32, (FB * 8, FB), 0) // 8
    fiber = lax.broadcasted_iota(jnp.int32, (FB * 8, FB), 1)
    where_s[...] = (group - fiber).astype(F32).astype(BF16)
    for c in sides:
        c.wait()
    for i in range(rows // SLAB_ROWS):
        band_s[0:BAND, i * SLAB_ROWS : (i + 1) * SLAB_ROWS] = bands_s[i]
    rt = row_matrix(band_s[...], offsets[0])
    rowmat_t[...] = rt
    rowmat[...] = rt.T
    for j in range(PW):
        pad_s[j : j + 1, 0:fib] = profile_s[j]
    start_s[0:1, 0:fib] = starts_s[...]
    lane = lax.broadcasted_iota(jnp.int32, (1, width), 1)
    jitter = start_s[0:1, :] - PITCH * lane
    base = pad_s[...]
    local = jnp.where(jitter == 0, base, 0.0)
    for d in range(1, 4):
        local = jnp.where(jitter == d, pltpu.roll(base, d, 0), local)
    low, high = local[0:8], local[8:16]
    nxt = pltpu.roll(low, width - 1, 1)

    def twice(x):
        return [jnp.concatenate([p.astype(F32)] * 2, 0).astype(BF16) for p in parts(x)]

    c_low, c_high = twice(low), twice(high)
    s_low, s_high = twice(low * low), twice(high * high)
    n_high = twice(high * nxt)
    edge_row = lax.broadcasted_iota(jnp.int32, (FB, FB), 0)
    edge_lane = lax.broadcasted_iota(jnp.int32, (FB, FB), 1)
    edge_on = ((edge_row < 8) & (edge_lane == FB - 1)).astype(F32).astype(BF16)
    zero = jnp.zeros((), BF16)

    def tall(x, cols, n):
        return jnp.broadcast_to(x[:, cols][None], (n // 16, 16, FB)).reshape(n, FB)

    def weights(c0, n):
        keep = 1.0 - mask_s[:, :, c0 : c0 + n].astype(F32)
        w = (inv_s[:, :, c0 : c0 + n] * keep).reshape(rows, n)
        return w, w * frames_s[:, :, c0 : c0 + n].reshape(rows, n)

    for c in copies[0]:
        c.wait()
    for b in range(blocks):
        cols = slice(b * FB, (b + 1) * FB)
        place = where_s[...]
        on, after = place == zero, place == jnp.ones((), BF16)

        def both(lows, highs):
            return [jnp.where(on, tall(x, cols, CB), jnp.where(after, tall(y, cols, CB), zero)) for x, y in zip(lows, highs)]

        square = both(s_low, s_high)
        cross = [jnp.where(after, tall(y, cols, CB), zero) for y in n_high]
        plain = both(c_low, c_high)
        pair = [jnp.concatenate([x, y], 1) for x, y in zip(square, cross)]
        w, v = weights(b * CB, CB)
        w = parts(w)
        v = parts(v)

        def products(w, v, pair, plain):
            t = mm(w[0], pair[0]) + mm(w[0], pair[1]) + mm(w[1], pair[0])
            t = t + mm(w[1], pair[1]) + mm(w[0], pair[2]) + mm(w[2], pair[0])
            two = jnp.concatenate(plain[0:2], 1)
            g = mm(v[0], two) + mm(v[1], two)
            g = g[:, 0:FB] + g[:, FB:] + mm(v[2], plain[0]) + mm(v[0], plain[2])
            return t[:, 0:FB], t[:, FB:], g

        tt, cc, gg = products(w, v, pair, plain)
        if b + 1 < blocks:
            for c in copies[b + 1]:
                c.wait()
            w, v = weights((b + 1) * CB, FB)
            edge_pair = [jnp.concatenate([tall(x, cols, FB) * edge_on, tall(y, cols, FB) * edge_on], 1) for x, y in zip(s_high, n_high)]
            edge_plain = [tall(x, cols, FB) * edge_on for x in c_high]
            et, ec, eg = products(parts(w), parts(v), edge_pair, edge_plain)
            tt, cc, gg = tt + et, cc + ec, gg + eg
        t0[:, cols] = tt
        t1[:, cols] = cc
        f[:, cols] = gg


def tri(t0, t1, u):
    width = u.shape[1]
    return t0 * u + t1 * pltpu.roll(u, width - 1, 1) + pltpu.roll(t1 * u, 1, 1)


def split(ext, parity, send_e, send_o, at):
    low, high = ext[0:HALF], ext[HALF:EXT]
    send_e[at : at + HALF, :] = jnp.where(parity == 0, high, low)
    send_o[at : at + HALF, :] = jnp.where(parity == 0, low, high)


def joined(part, got_e, got_o, parity, at):
    e, o = got_e[at : at + HALF, :], got_o[at : at + HALF, :]
    low = jnp.where(parity == 0, o, e)
    high = jnp.where(parity == 0, e, o)
    return jnp.concatenate([part[0:HALF, :] + low, part[HALF:EXT, :] + high], 0)


def lanes_of(x):
    s = jnp.sum(x, axis=0, keepdims=True)
    total = s[:, 0:LANES]
    for i in range(1, x.shape[1] // LANES):
        total = total + s[:, i * LANES : (i + 1) * LANES]
    return total


def own(x):
    return x[GHOST : GHOST + SLAB_ROWS, :]


def first_kernel(flux, flux_e, flux_o, t0, t1, f, rowmat, rowmat_t, start_ext, part, send_e, send_o, ext_s):
    parity = lax.rem(lax.axis_index("wave"), 2)
    fib = flux.shape[1]
    ext_s[...] = jnp.zeros_like(ext_s)
    cut = SLAB_ROWS - GHOST
    e, o = flux_e[...], flux_o[...]
    ext_s[0:GHOST, 0:fib] = jnp.where(parity == 0, o[cut:], e[cut:])
    ext_s[GHOST : GHOST + SLAB_ROWS, 0:fib] = flux[...]
    ext_s[GHOST + SLAB_ROWS : EXT, 0:fib] = jnp.where(parity == 0, e[0:GHOST], o[0:GHOST])
    r, rt = rowmat[...], rowmat_t[...]
    ext = ext_s[...]
    start_ext[...] = ext
    t = f[...] - tri(t0[...], t1[...], dot(r, ext))
    back = dot(rt, t)
    diag = dot(rt * rt, t0[...])
    part[0:EXT, :] = back
    part[EXT : 2 * EXT, :] = diag
    split(back, parity, send_e, send_o, 0)
    split(diag, parity, send_e, send_o, HALF)


def apply_rows(vec, rowmat, rowmat_t, t0, t1):
    u = dot(rowmat[...], vec)
    t = tri(t0[...], t1[...], u)
    return u, t, dot(rowmat_t[...], t)


def second_kernel(rowmat, rowmat_t, t0, t1, start_ext, part, got_e, got_o, diag, vec, mom, part_out, send_e, send_o):
    parity = lax.rem(lax.axis_index("wave"), 2)
    res = joined(part[0:EXT, :], got_e, got_o, parity, 0) - RIDGE * start_ext[...]
    d = joined(part[EXT : 2 * EXT, :], got_e, got_o, parity, HALF) + RIDGE
    p = res / d
    diag[...] = d
    vec[...] = p
    mom[...] = jnp.zeros_like(mom)
    mom[0:1, :] = lanes_of(own(p) * own(res))
    _, _, back = apply_rows(p, rowmat, rowmat_t, t0, t1)
    part_out[...] = back
    split(back, parity, send_e, send_o, 0)


def next_kernel(step, copies, rowmat, rowmat_t, t0, t1, diag, before, mom, part, got_e, got_o, vec, mom_out, part_out, send_e, send_o):
    parity = lax.rem(lax.axis_index("wave"), 2)
    prev = before[...]
    d = diag[...]
    image = joined(part, got_e, got_o, parity, 0) + RIDGE * prev
    p = image / d - SHIFT * prev
    vec[...] = p
    scaled = own(d) * own(p)
    u, t, back = apply_rows(p, rowmat, rowmat_t, t0, t1)
    part_out[...] = back
    split(back, parity, send_e, send_o, 0)
    moments = mom[...]
    row = lax.broadcasted_iota(jnp.int32, moments.shape, 0)
    new = [(2 * step - 1, lanes_of(scaled * own(prev))), (2 * step, lanes_of(scaled * own(p)))]
    if copies:
        new.append((2 * step + 1, lanes_of(u * t) + RIDGE * lanes_of(own(p) * own(p))))
    for i, value in new:
        moments = jnp.where(row == i, value, moments)
    if copies:
        mom_out[...] = jnp.broadcast_to(moments[None], mom_out.shape)
    else:
        mom_out[...] = moments


def coefficients(mom):
    mu = [mom[i : i + 1, :] for i in range(5)]
    nu = [mu[i + 1] + SHIFT * mu[i] for i in range(4)] + [mom[5:6, :]]

    def inner(p, w):
        total = None
        for i in range(len(p)):
            for j in range(len(p)):
                term = p[i] * p[j] * w[i + j]
                total = term if total is None else total + term
        return total

    one = jnp.ones_like(mu[0])
    rho, delta, energy = [one], [one], mu[0]
    chi = []
    for step in range(3):
        alpha = energy / inner(delta, nu)
        chi = [c + alpha * x for c, x in zip(chi + [0.0 * one], delta)]
        image = [SHIFT * x for x in delta] + [0.0 * one]
        image = [x + (delta[i - 1] if i else 0.0) for i, x in enumerate(image)]
        rho = [x - alpha * y for x, y in zip(rho + [0.0 * one], image)]
        if step < 2:
            fresh = inner(rho, mu)
            beta = fresh / energy
            delta = [x + beta * y for x, y in zip(rho, delta + [0.0 * one])]
            energy = fresh
    return chi, rho


def last_kernel(moms, diag, start_ext, p0, p1, p2, part, got_e, got_o, solution_ref, residual_ref):
    parity = lax.rem(lax.axis_index("wave"), 2)
    fib = solution_ref.shape[1]
    total = jnp.sum(moms[...], axis=0)
    total = jnp.broadcast_to(jnp.sum(total, axis=1, keepdims=True), total.shape)
    chi, rho = coefficients(total)
    width = diag.shape[1]

    def wide(c):
        return jnp.concatenate([c] * (width // LANES), 1)

    chi = [wide(c) for c in chi]
    rho = [wide(c) for c in rho]
    q0, q1, q2, d = own(p0), own(p1), own(p2), own(diag)
    image = own(joined(part, got_e, got_o, parity, 0)) + RIDGE * q2
    x = own(start_ext) + chi[0] * q0 + chi[1] * q1 + chi[2] * q2
    r = d * (rho[0] * q0 + rho[1] * q1 + rho[2] * q2) + rho[3] * (image - SHIFT * (d * q2))
    solution_ref[...] = x[:, 0:fib]
    residual_ref[...] = r[:, 0:fib]


def swap(values, pairs):
    return lax.ppermute(values, "wave", pairs)


def local(frames, inverse_var, masked, psf_band, offsets, starts, profile, flux_start):
    waves = lax.axis_size("wave")
    fib = flux_start.shape[1]
    expo, slab, columns = frames.shape
    rows = expo * slab
    blocks = columns // CB
    width = blocks * FB
    even = [(i, i ^ 1) for i in range(waves) if (i ^ 1) < waves]
    odd = [(i, j) for i in range(waves) for j in (((i + 1) ^ 1) - 1,) if 0 <= j < waves and j != i]

    flux_o, flux_e = swap(flux_start, odd), swap(flux_start, even)

    vm = pl.BlockSpec(memory_space=pltpu.VMEM)
    small = pltpu.CompilerParams(vmem_limit_bytes=VMEM_LIMIT)

    def shape(*dims):
        return jax.ShapeDtypeStruct(dims, F32)

    hb = pl.BlockSpec(memory_space=pltpu.HBM)
    sm = pl.BlockSpec(memory_space=pltpu.SMEM)
    raw = (offsets, starts, jnp.transpose(profile, (1, 0, 2)), jnp.transpose(psf_band, (0, 2, 1)), frames, inverse_var, masked)
    raw = [raw[0]] + [pltpu.with_memory_space_constraint(x, pltpu.HBM) for x in raw[1:]]
    t0, t1, f, rowmat, rowmat_t = pl.pallas_call(
        pixel_kernel,
        in_specs=[sm] + [hb] * 6,
        out_specs=[vm] * 5,
        out_shape=[shape(rows, width)] * 3 + [shape(rows, EXT), shape(EXT, rows)],
        scratch_shapes=[
            pltpu.VMEM(frames.shape, F32),
            pltpu.VMEM(frames.shape, F32),
            pltpu.VMEM(frames.shape, jnp.int32),
            pltpu.SemaphoreType.DMA((blocks, 3)),
            pltpu.VMEM((1, fib), jnp.int32),
            pltpu.VMEM((PW, 1, fib), F32),
            pltpu.VMEM((expo, BAND, slab), F32),
            pltpu.SemaphoreType.DMA((3,)),
            pltpu.VMEM((16, width), F32),
            pltpu.VMEM((8, width), jnp.int32),
            pltpu.VMEM((CB, FB), BF16),
            pltpu.VMEM((EXT, rows), F32),
        ],
        compiler_params=small,
        name="pixels",
    )(*raw)

    start_ext, part, send_e, send_o = pl.pallas_call(
        first_kernel,
        in_specs=[vm] * 8,
        out_specs=[vm] * 4,
        out_shape=[shape(EXT, width), shape(2 * EXT, width), shape(EXT, width), shape(EXT, width)],
        scratch_shapes=[pltpu.VMEM((EXT, width), F32)],
        compiler_params=small,
        name="first",
    )(flux_start, flux_e, flux_o, t0, t1, f, rowmat, rowmat_t)
    got_o, got_e = swap(send_o, odd), swap(send_e, even)

    diag, p0, mom, part, send_e, send_o = pl.pallas_call(
        second_kernel,
        in_specs=[vm] * 8,
        out_specs=[vm] * 6,
        out_shape=[shape(EXT, width), shape(EXT, width), shape(8, LANES), shape(EXT, width), shape(HALF, width), shape(HALF, width)],
        compiler_params=small,
        name="second",
    )(rowmat, rowmat_t, t0, t1, start_ext, part, got_e, got_o)
    vectors = [p0]
    for step in (1, 2):
        got_o, got_e = swap(send_o, odd), swap(send_e, even)
        copies = waves if step == 2 else 0
        mom_shape = shape(waves, 8, LANES) if copies else shape(8, LANES)
        vec, mom, part, send_e, send_o = pl.pallas_call(
            functools.partial(next_kernel, step, copies),
            in_specs=[vm] * 10,
            out_specs=[vm] * 5,
            out_shape=[shape(EXT, width), mom_shape, shape(EXT, width), shape(HALF, width), shape(HALF, width)],
            compiler_params=small,
            name=f"next{step}",
        )(rowmat, rowmat_t, t0, t1, diag, vectors[-1], mom, part, got_e, got_o)
        vectors.append(vec)
    got_o, got_e = swap(send_o, odd), swap(send_e, even)
    moms = lax.all_to_all(mom, "wave", 0, 0)
    return tuple(
        pl.pallas_call(
            last_kernel,
            in_specs=[vm] * 9,
            out_specs=[vm] * 2,
            out_shape=[shape(slab, fib)] * 2,
            compiler_params=small,
        name="last",
        )(moms, diag, start_ext, *vectors, part, got_e, got_o)
    )


def solution(mesh):
    placed = (
        P(None, ("tile", "wave"), None),
        P(None, ("tile", "wave"), None),
        P(None, ("tile", "wave"), None),
        P(None, ("tile", "wave"), None),
        P(("tile", "wave")),
        P(("tile", "wave"), None),
        P(("tile", "wave"), None, None),
        P(("tile", "wave"), None),
    )
    return jax.shard_map(
        local,
        mesh=mesh,
        in_specs=placed,
        out_specs=(P(("tile", "wave"), None), P(("tile", "wave"), None)),
        check_vma=False,
    )
```

time: 71.2 us -> 52.5 us (0.74)
  Pallas kernels: 23 us -> 12.6 us
  local copies, waits for them, and re-layouts: 6.04 us -> 0.01 us
  other arithmetic: 1.44 us -> 0 us
  waiting for transfers between devices: 7.61 us -> 6.64 us
    pallas_call x6, Pallas kernels: 23 us -> 12.6 us  [the longest x1 7.92 us: local(): pl.pallas_call(pixel_kernel, in_specs=[sm] + [hb] * 6, out_specs=[vm] * 5...]
    unnamed x24 -> x2, local copies, waits for them, and re-layouts: 6.04 us -> 0.01 us
    ppermute x10, waiting for transfers between devices: 2.25 us -> 1.12 us  [swap(): return lax.ppermute(values, 'wave', pairs)]
    select_n x1 -> x0, other arithmetic: 0.78 us -> none  [local(): flux_o = swap(jnp.where(parity == 0, first, last), odd)]
  transfers between devices with their start and end apart: 11 -> 11, of which waited for: 5 -> 5; matrix products, arithmetic and copies ran while one was open for 5% -> 0% of each run, Pallas kernels for 13% -> 15%
where the time goes in v1:
time: 52.5 us; the launch traced here: 52.2 us
  starting transfers between devices  31.6 us (60%)
  Pallas kernels  12.6 us (24%)
  waiting for transfers between devices  6.64 us (13%)
  between operations  1.4 us (3%)
    ppermute x10, starting transfers between devices, swap(): return lax.ppermute(values, 'wave', pairs)  19.6 us
    all_to_all x1, starting transfers between devices, local(): moms = lax.all_to_all(mom, 'wave', 0, 0)  12 us
    pallas_call x1, Pallas kernels, local(): pl.pallas_call(pixel_kernel, in_specs=[sm] + [hb] * 6, out_specs=[vm] * 5...  7.92 us
    all_to_all x1, waiting for transfers between devices, local(): moms = lax.all_to_all(mom, 'wave', 0, 0)  5.52 us
    pallas_call x2, Pallas kernels, local(): pl.pallas_call(functools.partial(next_kernel, step, copies), in_specs=[vm...  2.07 us
    ppermute x10, waiting for transfers between devices, swap(): return lax.ppermute(values, 'wave', pairs)  1.12 us
  transfers between devices with their start and end apart: 11, of which 5 were waited for; matrix products, arithmetic and copies ran while one was open for 0% of the time, Pallas kernels for 15%

profile of v1, /device:TPU:0, one launch (start us, length us, event | category | flops | bytes accessed | tf_op | source)
XLA Modules:
  0.0 52.2 jit_solution(15434377912324931501)
XLA Ops:
  0.6 0.6 %collective-permute-start = (f32[32,500]{1,0:T(8,128)}, f32[32,500]{1,0:T(8,128)S(1)}, u32[]{:S(2)}, u32[]{:S(2)}) collective-permute-start(f32[32,500]{1,0:T(8,128)} %flux.1), channel_id=1, source_target_pairs={{0,1},{1,0},{2,3},{3,2},{4,5},{5,4},{6,7},{7,6},{8,9},{9,8},{10,11... | collective-permute-start | bytes 192008 | tf_op jit(solution)/shard_map/ppermute | solution.py:308
  1.2 0.7 %collective-permute-start.1 = (f32[32,500]{1,0:T(8,128)}, f32[32,500]{1,0:T(8,128)S(1)}, u32[]{:S(2)}, u32[]{:S(2)}) collective-permute-start(f32[32,500]{1,0:T(8,128)} %flux.1), channel_id=1, source_target_pairs={{1,2},{2,1},{3,4},{4,3},{5,6},{6,5},{7,8},{8,7},{9,10},{10,9},{11,... | collective-permute-start | bytes 192008 | tf_op jit(solution)/shard_map/ppermute | solution.py:308
  2.5 0.0 copy-start
  2.5 7.9 %pixels.1 = (f32[128,512]{1,0:T(8,128)S(1)}, f32[128,512]{1,0:T(8,128)S(1)}, f32[128,512]{1,0:T(8,128)S(1)}, f32[128,64]{1,0:T(8,128)S(1)}, f32[64,128]{1,0:T(8,128)S(1)}) custom-call(s32[1]{0:T(128)S(6)} %copy.10.offsets, s32[1,500]{1,0:T(1,128)} %starts.1, f32[12,1,500]{2,1,0:T(1,128)} %bitcast.3, f32[4,16,32]{2,1,0:T(8,128)} %bitcast.2, ...), custom_call_target="tpu_custom_call" | custom-call | tf_op jit(solution)/shard_map/pixels/pallas_call | solution.py:333
  10.4 0.0 collective-permute-done.flux_e
  10.4 0.0 collective-permute-done.1.flux_o
  10.5 0.0 copy-done
  10.5 0.9 %first.1 = (f32[64,512]{1,0:T(8,128)S(1)}, f32[128,512]{1,0:T(8,128)S(1)}, f32[64,512]{1,0:T(8,128)S(1)}, f32[64,512]{1,0:T(8,128)S(1)}) custom-call(f32[32,500]{1,0:T(8,128)S(1)} %copy-done, f32[32,500]{1,0:T(8,128)S(1)} %collective-permute-done.flux_e, f32[32,500]{1,0:T(8,128)S(1)} %collective-permute-done.1.flux_o, f32[128,512]{1,0:T(8,128)S(1)} %get-tuple-element.29.t0, ...), custom_call_target="tpu_custom_call" | custom-call | tf_op jit(solution)/shard_map/first/pallas_call | solution.py:356
  11.4 3.9 %collective-permute-start.2 = (f32[64,512]{1,0:T(8,128)S(1)}, f32[64,512]{1,0:T(8,128)S(1)}, u32[]{:S(2)}, u32[]{:S(2)}) collective-permute-start(f32[64,512]{1,0:T(8,128)S(1)} %get-tuple-element.34), channel_id=1, source_target_pairs={{0,1},{1,0},{2,3},{3,2},{4,5},{5,4},{6,7},{7,6},{8,9},{9,8},{10,11... | collective-permute-start | bytes 393224 | tf_op jit(solution)/shard_map/ppermute | solution.py:308
  15.3 0.7 %collective-permute-start.3 = (f32[64,512]{1,0:T(8,128)S(1)}, f32[64,512]{1,0:T(8,128)S(1)}, u32[]{:S(2)}, u32[]{:S(2)}) collective-permute-start(f32[64,512]{1,0:T(8,128)S(1)} %get-tuple-element.35), channel_id=1, source_target_pairs={{1,2},{2,1},{3,4},{4,3},{5,6},{6,5},{7,8},{8,7},{9,10},{10,9},{11,... | collective-permute-start | bytes 393224 | tf_op jit(solution)/shard_map/ppermute | solution.py:308
  16.0 0.3 collective-permute-done.2.got_e
  16.3 0.0 collective-permute-done.3.got_o
  16.3 0.8 %second.1 = (f32[64,512]{1,0:T(8,128)S(1)}, f32[64,512]{1,0:T(8,128)S(1)}, f32[8,128]{1,0:T(8,128)S(1)}, f32[64,512]{1,0:T(8,128)S(1)}, f32[32,512]{1,0:T(8,128)S(1)}, /*index=5*/f32[32,512]{1,0:T(8,128)S(1)}) custom-call(f32[128,64]{1,0:T(8,128)S(1)} %get-tuple-element.27.rowmat, f32[64,128]{1,0:T(8,128)S(1)} %get-tuple-element.28.rowmat_t, ...), custom_call_target="tpu_custom_call" | custom-call | tf_op jit(solution)/shard_map/second/pallas_call | solution.py:367
  17.1 5.4 %collective-permute-start.4 = (f32[32,512]{1,0:T(8,128)S(1)}, f32[32,512]{1,0:T(8,128)S(1)}, u32[]{:S(2)}, u32[]{:S(2)}) collective-permute-start(f32[32,512]{1,0:T(8,128)S(1)} %get-tuple-element.40), channel_id=1, source_target_pairs={{0,1},{1,0},{2,3},{3,2},{4,5},{5,4},{6,7},{7,6},{8,9},{9,8},{10,11... | collective-permute-start | bytes 196616 | tf_op jit(solution)/shard_map/ppermute | solution.py:308
  22.5 0.7 %collective-permute-start.5 = (f32[32,512]{1,0:T(8,128)S(1)}, f32[32,512]{1,0:T(8,128)S(1)}, u32[]{:S(2)}, u32[]{:S(2)}) collective-permute-start(f32[32,512]{1,0:T(8,128)S(1)} %get-tuple-element.41), channel_id=1, source_target_pairs={{1,2},{2,1},{3,4},{4,3},{5,6},{6,5},{7,8},{8,7},{9,10},{10,9},{11,... | collective-permute-start | bytes 196616 | tf_op jit(solution)/shard_map/ppermute | solution.py:308
  23.2 0.2 collective-permute-done.4.got_e
  23.4 0.0 collective-permute-done.5.got_o
  23.4 0.8 %next1.1 = (f32[64,512]{1,0:T(8,128)S(1)}, f32[8,128]{1,0:T(8,128)S(1)}, f32[64,512]{1,0:T(8,128)S(1)}, f32[32,512]{1,0:T(8,128)S(1)}, f32[32,512]{1,0:T(8,128)S(1)}) custom-call(f32[128,64]{1,0:T(8,128)S(1)} %get-tuple-element.27.rowmat, f32[64,128]{1,0:T(8,128)S(1)} %get-tuple-element.28.rowmat_t, f32[128,512]{1,0:T(8,128)S(1)} %get-tuple-element.29.t0, ...), custom_call_target="tpu_custom_call" | custom-call | tf_op jit(solution)/shard_map/next1/pallas_call | solution.py:380
  24.3 6.1 %collective-permute-start.6 = (f32[32,512]{1,0:T(8,128)S(1)}, f32[32,512]{1,0:T(8,128)S(1)}, u32[]{:S(2)}, u32[]{:S(2)}) collective-permute-start(f32[32,512]{1,0:T(8,128)S(1)} %get-tuple-element.45), channel_id=1, source_target_pairs={{0,1},{1,0},{2,3},{3,2},{4,5},{5,4},{6,7},{7,6},{8,9},{9,8},{10,11... | collective-permute-start | bytes 196616 | tf_op jit(solution)/shard_map/ppermute | solution.py:308
  30.3 0.7 %collective-permute-start.7 = (f32[32,512]{1,0:T(8,128)S(1)}, f32[32,512]{1,0:T(8,128)S(1)}, u32[]{:S(2)}, u32[]{:S(2)}) collective-permute-start(f32[32,512]{1,0:T(8,128)S(1)} %get-tuple-element.46), channel_id=1, source_target_pairs={{1,2},{2,1},{3,4},{4,3},{5,6},{6,5},{7,8},{8,7},{9,10},{10,9},{11,... | collective-permute-start | bytes 196616 | tf_op jit(solution)/shard_map/ppermute | solution.py:308
  31.0 0.2 collective-permute-done.6.got_e
  31.2 0.0 collective-permute-done.7.got_o
  31.2 1.2 %next2.1 = (f32[64,512]{1,0:T(8,128)S(1)}, f32[16,8,128]{2,1,0:T(8,128)}, f32[64,512]{1,0:T(8,128)S(1)}, f32[32,512]{1,0:T(8,128)S(1)}, f32[32,512]{1,0:T(8,128)S(1)}) custom-call(f32[128,64]{1,0:T(8,128)S(1)} %get-tuple-element.27.rowmat, f32[64,128]{1,0:T(8,128)S(1)} %get-tuple-element.28.rowmat_t, f32[128,512]{1,0:T(8,128)S(1)} %get-tuple-element.29.t0, ...), custom_call_target="tpu_custom_call" | custom-call | tf_op jit(solution)/shard_map/next2/pallas_call | solution.py:380
  32.5 12.0 %all-to-all-start = ((f32[16,8,128]{2,1,0:T(8,128)}), f32[16,8,128]{2,1,0:T(8,128)S(1)}, u32[]{:S(2)}, u32[]{:S(2)}) async-start(f32[16,8,128]{2,1,0:T(8,128)} %get-tuple-element.47), calls=%async_computation | async-start | bytes 131072 | tf_op jit(solution)/shard_map/all_to_all | solution.py:390
  44.5 0.4 collective-permute-start.8
  44.9 0.7 %collective-permute-start.9 = (f32[32,512]{1,0:T(8,128)S(1)}, f32[32,512]{1,0:T(8,128)S(1)}, u32[]{:S(2)}, u32[]{:S(2)}) collective-permute-start(f32[32,512]{1,0:T(8,128)S(1)} %get-tuple-element.51), channel_id=1, source_target_pairs={{1,2},{2,1},{3,4},{4,3},{5,6},{6,5},{7,8},{8,7},{9,10},{10,9},{11,... | collective-permute-start | bytes 196616 | tf_op jit(solution)/shard_map/ppermute | solution.py:308
  45.6 0.3 collective-permute-done.8.got_e
  45.9 0.0 collective-permute-done.9.got_o
  45.9 5.5 %all-to-all-done.moms = f32[16,8,128]{2,1,0:T(8,128)S(1)} async-done(((f32[16,8,128]{2,1,0:T(8,128)}), f32[16,8,128]{2,1,0:T(8,128)S(1)}, u32[]{:S(2)}, u32[]{:S(2)}) %all-to-all-start) | async-done | bytes 65568 | tf_op jit(solution)/shard_map/all_to_all | solution.py:390
  51.4 0.8 %last.1 = (f32[32,500]{1,0:T(8,128)}, f32[32,500]{1,0:T(8,128)}) custom-call(f32[16,8,128]{2,1,0:T(8,128)S(1)} %all-to-all-done.moms, f32[64,512]{1,0:T(8,128)S(1)} %get-tuple-element.36.diag, f32[64,512]{1,0:T(8,128)S(1)} %get-tuple-element.32.start_ext, f32[64,512]{1,0:T(8,128)S(1)} %get-tuple-element.37.before.p0, ...), custom_call_target="tpu_custom_call" | custom-call | tf_op jit(solution)/shard_map/last/pallas_call | solution.py:392
Async XLA Ops:
  0.6 9.8 %collective-permute-start = (f32[32,500]{1,0:T(8,128)}, f32[32,500]{1,0:T(8,128)S(1)}, u32[]{:S(2)}, u32[]{:S(2)}) collective-permute-start(f32[32,500]{1,0:T(8,128)} %flux.1), channel_id=1, source_target_pairs={{0,1},{1,0},{2,3},{3,2},{4,5},{5,4},{6,7},{7,6},{8,9},{9,8},{10,11... | collective-permute-start | bytes 192008 | tf_op jit(solution)/shard_map/ppermute | solution.py:308
  1.2 9.3 %collective-permute-start.1 = (f32[32,500]{1,0:T(8,128)}, f32[32,500]{1,0:T(8,128)S(1)}, u32[]{:S(2)}, u32[]{:S(2)}) collective-permute-start(f32[32,500]{1,0:T(8,128)} %flux.1), channel_id=1, source_target_pairs={{1,2},{2,1},{3,4},{4,3},{5,6},{6,5},{7,8},{8,7},{9,10},{10,9},{11,... | collective-permute-start | bytes 192008 | tf_op jit(solution)/shard_map/ppermute | solution.py:308
  2.5 8.0 %copy-start = (f32[32,500]{1,0:T(8,128)S(1)}, f32[32,500]{1,0:T(8,128)}, u32[]{:S(2)}) copy-start(f32[32,500]{1,0:T(8,128)} %flux.1) | copy-start | bytes 192004
  11.4 4.9 %collective-permute-start.2 = (f32[64,512]{1,0:T(8,128)S(1)}, f32[64,512]{1,0:T(8,128)S(1)}, u32[]{:S(2)}, u32[]{:S(2)}) collective-permute-start(f32[64,512]{1,0:T(8,128)S(1)} %get-tuple-element.34), channel_id=1, source_target_pairs={{0,1},{1,0},{2,3},{3,2},{4,5},{5,4},{6,7},{7,6},{8,9},{9,8},{10,11... | collective-permute-start | bytes 393224 | tf_op jit(solution)/shard_map/ppermute | solution.py:308
  15.3 1.0 %collective-permute-start.3 = (f32[64,512]{1,0:T(8,128)S(1)}, f32[64,512]{1,0:T(8,128)S(1)}, u32[]{:S(2)}, u32[]{:S(2)}) collective-permute-start(f32[64,512]{1,0:T(8,128)S(1)} %get-tuple-element.35), channel_id=1, source_target_pairs={{1,2},{2,1},{3,4},{4,3},{5,6},{6,5},{7,8},{8,7},{9,10},{10,9},{11,... | collective-permute-start | bytes 393224 | tf_op jit(solution)/shard_map/ppermute | solution.py:308
  17.1 6.3 %collective-permute-start.4 = (f32[32,512]{1,0:T(8,128)S(1)}, f32[32,512]{1,0:T(8,128)S(1)}, u32[]{:S(2)}, u32[]{:S(2)}) collective-permute-start(f32[32,512]{1,0:T(8,128)S(1)} %get-tuple-element.40), channel_id=1, source_target_pairs={{0,1},{1,0},{2,3},{3,2},{4,5},{5,4},{6,7},{7,6},{8,9},{9,8},{10,11... | collective-permute-start | bytes 196616 | tf_op jit(solution)/shard_map/ppermute | solution.py:308
  22.5 0.9 %collective-permute-start.5 = (f32[32,512]{1,0:T(8,128)S(1)}, f32[32,512]{1,0:T(8,128)S(1)}, u32[]{:S(2)}, u32[]{:S(2)}) collective-permute-start(f32[32,512]{1,0:T(8,128)S(1)} %get-tuple-element.41), channel_id=1, source_target_pairs={{1,2},{2,1},{3,4},{4,3},{5,6},{6,5},{7,8},{8,7},{9,10},{10,9},{11,... | collective-permute-start | bytes 196616 | tf_op jit(solution)/shard_map/ppermute | solution.py:308
  24.3 7.0 %collective-permute-start.6 = (f32[32,512]{1,0:T(8,128)S(1)}, f32[32,512]{1,0:T(8,128)S(1)}, u32[]{:S(2)}, u32[]{:S(2)}) collective-permute-start(f32[32,512]{1,0:T(8,128)S(1)} %get-tuple-element.45), channel_id=1, source_target_pairs={{0,1},{1,0},{2,3},{3,2},{4,5},{5,4},{6,7},{7,6},{8,9},{9,8},{10,11... | collective-permute-start | bytes 196616 | tf_op jit(solution)/shard_map/ppermute | solution.py:308
  30.3 0.9 %collective-permute-start.7 = (f32[32,512]{1,0:T(8,128)S(1)}, f32[32,512]{1,0:T(8,128)S(1)}, u32[]{:S(2)}, u32[]{:S(2)}) collective-permute-start(f32[32,512]{1,0:T(8,128)S(1)} %get-tuple-element.46), channel_id=1, source_target_pairs={{1,2},{2,1},{3,4},{4,3},{5,6},{6,5},{7,8},{8,7},{9,10},{10,9},{11,... | collective-permute-start | bytes 196616 | tf_op jit(solution)/shard_map/ppermute | solution.py:308
  32.5 18.9 %all-to-all-start = ((f32[16,8,128]{2,1,0:T(8,128)}), f32[16,8,128]{2,1,0:T(8,128)S(1)}, u32[]{:S(2)}, u32[]{:S(2)}) async-start(f32[16,8,128]{2,1,0:T(8,128)} %get-tuple-element.47), calls=%async_computation | async-start | bytes 131072 | tf_op jit(solution)/shard_map/all_to_all | solution.py:390
  44.5 1.4 %collective-permute-start.8 = (f32[32,512]{1,0:T(8,128)S(1)}, f32[32,512]{1,0:T(8,128)S(1)}, u32[]{:S(2)}, u32[]{:S(2)}) collective-permute-start(f32[32,512]{1,0:T(8,128)S(1)} %get-tuple-element.50), channel_id=1, source_target_pairs={{0,1},{1,0},{2,3},{3,2},{4,5},{5,4},{6,7},{7,6},{8,9},{9,8},{10,11... | collective-permute-start | bytes 196616 | tf_op jit(solution)/shard_map/ppermute | solution.py:308
  44.9 1.0 %collective-permute-start.9 = (f32[32,512]{1,0:T(8,128)S(1)}, f32[32,512]{1,0:T(8,128)S(1)}, u32[]{:S(2)}, u32[]{:S(2)}) collective-permute-start(f32[32,512]{1,0:T(8,128)S(1)} %get-tuple-element.51), channel_id=1, source_target_pairs={{1,2},{2,1},{3,4},{4,3},{5,6},{6,5},{7,8},{8,7},{9,10},{10,9},{11,... | collective-permute-start | bytes 196616 | tf_op jit(solution)/shard_map/ppermute | solution.py:308

commit v2 on v1

--- a/solution.py
+++ b/solution.py
@@ -54,14 +54,14 @@
 
 
 def pixel_kernel(offsets, starts, profile, band, frames, inverse_var, masked, t0, t1, f, rowmat, rowmat_t,
-                 frames_s, inv_s, mask_s, sems, starts_s, profile_s, bands_s, side_sems, pad_s, start_s, where_s, band_s):
+                 frames_s, inv_s, mask_s, sems, starts_s, profile_s, bands_s, side_sems, pad_s, start_s, band_s):
     fib = starts.shape[1]
     rows, width = t0.shape
-    sides = [
+    side_copies = [
         pltpu.make_async_copy(src, dst, side_sems.at[i])
         for i, (src, dst) in enumerate(((starts, starts_s), (profile, profile_s), (band, bands_s)))
     ]
-    for c in sides:
+    for c in side_copies:
         c.start()
     blocks = width // FB
     copies = []
@@ -71,20 +71,18 @@
             pltpu.make_async_copy(src.at[:, :, cols], dst.at[:, :, cols], sems.at[b, i])
             for i, (src, dst) in enumerate(((inverse_var, inv_s), (masked, mask_s), (frames, frames_s)))
         ])
-    for group in copies:
-        for c in group:
-            c.start()
+    for c in copies[0]:
+        c.start()
 
     pad_s[...] = jnp.zeros_like(pad_s)
     start_s[...] = jnp.zeros_like(start_s)
     band_s[...] = jnp.zeros_like(band_s)
-    group = lax.broadcasted_iota(jnp.int32, (FB * 8, FB), 0) // 8
-    fiber = lax.broadcasted_iota(jnp.int32, (FB * 8, FB), 1)
-    where_s[...] = (group - fiber).astype(F32).astype(BF16)
-    for c in sides:
+    for c in side_copies:
         c.wait()
     for i in range(rows // SLAB_ROWS):
         band_s[0:BAND, i * SLAB_ROWS : (i + 1) * SLAB_ROWS] = bands_s[i]
+    for c in copies[1]:
+        c.start()
     rt = row_matrix(band_s[...], offsets[0])
     rowmat_t[...] = rt
     rowmat[...] = rt.T
@@ -106,57 +104,64 @@
     c_low, c_high = twice(low), twice(high)
     s_low, s_high = twice(low * low), twice(high * high)
     n_high = twice(high * nxt)
-    edge_row = lax.broadcasted_iota(jnp.int32, (FB, FB), 0)
-    edge_lane = lax.broadcasted_iota(jnp.int32, (FB, FB), 1)
-    edge_on = ((edge_row < 8) & (edge_lane == FB - 1)).astype(F32).astype(BF16)
-    zero = jnp.zeros((), BF16)
-
-    def tall(x, cols, n):
-        return jnp.broadcast_to(x[:, cols][None], (n // 16, 16, FB)).reshape(n, FB)
-
-    def weights(c0, n):
-        keep = 1.0 - mask_s[:, :, c0 : c0 + n].astype(F32)
-        w = (inv_s[:, :, c0 : c0 + n] * keep).reshape(rows, n)
-        return w, w * frames_s[:, :, c0 : c0 + n].reshape(rows, n)
-
-    for c in copies[0]:
-        c.wait()
+    zero = jnp.zeros((16, FB), BF16)
+    lane = lax.broadcasted_iota(jnp.int32, (16, FB), 1) - lax.broadcasted_iota(jnp.int32, (16, FB), 0) // 8
+    lane = lane.astype(F32).astype(BF16)
+    edge = (lax.broadcasted_iota(jnp.int32, (16, FB), 1) == FB - 1) & (lax.broadcasted_iota(jnp.int32, (16, FB), 0) < 8)
+    edge = edge.astype(F32).astype(BF16)
+
+    def expand(b):
+        cols = slice(b * FB, (b + 1) * FB)
+        cl, ch = [x[:, cols] for x in c_low], [x[:, cols] for x in c_high]
+        sl, sh = [x[:, cols] for x in s_low], [x[:, cols] for x in s_high]
+        nh = [x[:, cols] for x in n_high]
+        square, cross, plain = ([[], [], []] for _ in range(3))
+        for t in range(CB // 16):
+            on = lane == jnp.asarray(2 * t, BF16)
+            after = lane == jnp.asarray(2 * t - 1, BF16)
+            for i in range(3):
+                square[i].append(jnp.where(on, sl[i], jnp.where(after, sh[i], zero)))
+                cross[i].append(jnp.where(after, nh[i], zero))
+                plain[i].append(jnp.where(on, cl[i], jnp.where(after, ch[i], zero)))
+        return [[jnp.concatenate(x, 0) for x in group] for group in (square, cross, plain)]
+
+    def products(w, v, square, cross, plain):
+        pair = [jnp.concatenate([x, y], 1) for x, y in zip(square, cross)]
+        t = mm(jnp.concatenate(w, 0), pair[0])
+        g = mm(jnp.concatenate(w[0:2], 0), pair[1])
+        t = t[0:rows] + t[rows : 2 * rows] + t[2 * rows :] + g[0:rows] + g[rows:] + mm(w[0], pair[2])
+        g = mm(jnp.concatenate(v, 0), jnp.concatenate(plain[0:2], 1))
+        g = g[0:rows] + g[rows : 2 * rows] + g[2 * rows :]
+        g = g[:, 0:FB] + g[:, FB:] + mm(v[0], plain[2])
+        return t[:, 0:FB], t[:, FB:], g
+
     for b in range(blocks):
+        for c in copies[b]:
+            c.wait()
+        if b + 2 < blocks:
+            for c in copies[b + 2]:
+                c.start()
+        at = slice(b * CB, (b + 1) * CB)
+        w = (inv_s[:, :, at] * (1.0 - mask_s[:, :, at].astype(F32))).reshape(rows, CB)
+        v = w * frames_s[:, :, at].reshape(rows, CB)
+        w, v = parts(w), parts(v)
+        tt, cc, gg = products(w, v, *expand(b))
         cols = slice(b * FB, (b + 1) * FB)
-        place = where_s[...]
-        on, after = place == zero, place == jnp.ones((), BF16)
-
-        def both(lows, highs):
-            return [jnp.where(on, tall(x, cols, CB), jnp.where(after, tall(y, cols, CB), zero)) for x, y in zip(lows, highs)]
-
-        square = both(s_low, s_high)
-        cross = [jnp.where(after, tall(y, cols, CB), zero) for y in n_high]
-        plain = both(c_low, c_high)
-        pair = [jnp.concatenate([x, y], 1) for x, y in zip(square, cross)]
-        w, v = weights(b * CB, CB)
-        w = parts(w)
-        v = parts(v)
-
-        def products(w, v, pair, plain):
-            t = mm(w[0], pair[0]) + mm(w[0], pair[1]) + mm(w[1], pair[0])
-            t = t + mm(w[1], pair[1]) + mm(w[0], pair[2]) + mm(w[2], pair[0])
-            two = jnp.concatenate(plain[0:2], 1)
-            g = mm(v[0], two) + mm(v[1], two)
-            g = g[:, 0:FB] + g[:, FB:] + mm(v[2], plain[0]) + mm(v[0], plain[2])
-            return t[:, 0:FB], t[:, FB:], g
-
-        tt, cc, gg = products(w, v, pair, plain)
-        if b + 1 < blocks:
-            for c in copies[b + 1]:
-                c.wait()
-            w, v = weights((b + 1) * CB, FB)
-            edge_pair = [jnp.concatenate([tall(x, cols, FB) * edge_on, tall(y, cols, FB) * edge_on], 1) for x, y in zip(s_high, n_high)]
-            edge_plain = [tall(x, cols, FB) * edge_on for x in c_high]
-            et, ec, eg = products(parts(w), parts(v), edge_pair, edge_plain)
-            tt, cc, gg = tt + et, cc + ec, gg + eg
         t0[:, cols] = tt
         t1[:, cols] = cc
         f[:, cols] = gg
+        if b > 0:
+            cols = slice((b - 1) * FB, b * FB)
+            below = jnp.zeros((FB - 16, FB), BF16)
+
+            def tip(x):
+                return jnp.concatenate([x[:, cols] * edge, below], 0)
+
+            tips = [[tip(x) for x in group] for group in (s_high, n_high, c_high)]
+            tt, cc, gg = products([x[:, 0:FB] for x in w], [x[:, 0:FB] for x in v], *tips)
+            t0[:, cols] += tt
+            t1[:, cols] += cc
+            f[:, cols] += gg
 
 
 def tri(t0, t1, u):
@@ -170,10 +175,15 @@
     send_o[at : at + HALF, :] = jnp.where(parity == 0, low, high)
 
 
-def joined(part, got_e, got_o, parity, at):
-    e, o = got_e[at : at + HALF, :], got_o[at : at + HALF, :]
-    low = jnp.where(parity == 0, o, e)
-    high = jnp.where(parity == 0, e, o)
+def sides(e, o):
+    index, last = lax.axis_index("wave"), lax.axis_size("wave") - 1
+    even = lax.rem(index, 2) == 0
+    low = jnp.where(index == 0, 0.0, jnp.where(even, o, e))
+    return low, jnp.where(index == last, 0.0, jnp.where(even, e, o))
+
+
+def joined(part, got_e, got_o, at):
+    low, high = sides(got_e[at : at + HALF, :], got_o[at : at + HALF, :])
     return jnp.concatenate([part[0:HALF, :] + low, part[HALF:EXT, :] + high], 0)
 
 
@@ -193,11 +203,10 @@
     parity = lax.rem(lax.axis_index("wave"), 2)
     fib = flux.shape[1]
     ext_s[...] = jnp.zeros_like(ext_s)
-    cut = SLAB_ROWS - GHOST
-    e, o = flux_e[...], flux_o[...]
-    ext_s[0:GHOST, 0:fib] = jnp.where(parity == 0, o[cut:], e[cut:])
+    low, high = sides(flux_e[...], flux_o[...])
+    ext_s[0:GHOST, 0:fib] = low[SLAB_ROWS - GHOST :]
     ext_s[GHOST : GHOST + SLAB_ROWS, 0:fib] = flux[...]
-    ext_s[GHOST + SLAB_ROWS : EXT, 0:fib] = jnp.where(parity == 0, e[0:GHOST], o[0:GHOST])
+    ext_s[GHOST + SLAB_ROWS : EXT, 0:fib] = high[0:GHOST]
     r, rt = rowmat[...], rowmat_t[...]
     ext = ext_s[...]
     start_ext[...] = ext
@@ -218,8 +227,8 @@
 
 def second_kernel(rowmat, rowmat_t, t0, t1, start_ext, part, got_e, got_o, diag, vec, mom, part_out, send_e, send_o):
     parity = lax.rem(lax.axis_index("wave"), 2)
-    res = joined(part[0:EXT, :], got_e, got_o, parity, 0) - RIDGE * start_ext[...]
-    d = joined(part[EXT : 2 * EXT, :], got_e, got_o, parity, HALF) + RIDGE
+    res = joined(part[0:EXT, :], got_e, got_o, 0) - RIDGE * start_ext[...]
+    d = joined(part[EXT : 2 * EXT, :], got_e, got_o, HALF) + RIDGE
     p = res / d
     diag[...] = d
     vec[...] = p
@@ -234,7 +243,7 @@
     parity = lax.rem(lax.axis_index("wave"), 2)
     prev = before[...]
     d = diag[...]
-    image = joined(part, got_e, got_o, parity, 0) + RIDGE * prev
+    image = joined(part, got_e, got_o, 0) + RIDGE * prev
     p = image / d - SHIFT * prev
     vec[...] = p
     scaled = own(d) * own(p)
@@ -284,7 +293,6 @@
 
 
 def last_kernel(moms, diag, start_ext, p0, p1, p2, part, got_e, got_o, solution_ref, residual_ref):
-    parity = lax.rem(lax.axis_index("wave"), 2)
     fib = solution_ref.shape[1]
     total = jnp.sum(moms[...], axis=0)
     total = jnp.broadcast_to(jnp.sum(total, axis=1, keepdims=True), total.shape)
@@ -297,15 +305,28 @@
     chi = [wide(c) for c in chi]
     rho = [wide(c) for c in rho]
     q0, q1, q2, d = own(p0), own(p1), own(p2), own(diag)
-    image = own(joined(part, got_e, got_o, parity, 0)) + RIDGE * q2
+    image = own(joined(part, got_e, got_o, 0)) + RIDGE * q2
     x = own(start_ext) + chi[0] * q0 + chi[1] * q1 + chi[2] * q2
     r = d * (rho[0] * q0 + rho[1] * q1 + rho[2] * q2) + rho[3] * (image - SHIFT * (d * q2))
     solution_ref[...] = x[:, 0:fib]
     residual_ref[...] = r[:, 0:fib]
 
 
+def partners(tiles, waves):
+    even, odd = [], []
+    for tile in range(tiles):
+        for i in range(waves):
+            here = tile * waves + i
+            for found, other in ((even, i ^ 1), (odd, ((i + 1) ^ 1) - 1)):
+                if 0 <= other < waves:
+                    found.append((here, tile * waves + other))
+                elif tile ^ 1 < tiles:
+                    found.append((here, (tile ^ 1) * waves + i))
+    return even, odd
+
+
 def swap(values, pairs):
-    return lax.ppermute(values, "wave", pairs)
+    return lax.ppermute(values, ("tile", "wave"), pairs)
 
 
 def local(frames, inverse_var, masked, psf_band, offsets, starts, profile, flux_start):
@@ -315,9 +336,7 @@
     rows = expo * slab
     blocks = columns // CB
     width = blocks * FB
-    even = [(i, i ^ 1) for i in range(waves) if (i ^ 1) < waves]
-    odd = [(i, j) for i in range(waves) for j in (((i + 1) ^ 1) - 1,) if 0 <= j < waves and j != i]
-
+    even, odd = partners(lax.axis_size("tile"), waves)
     flux_o, flux_e = swap(flux_start, odd), swap(flux_start, even)
 
     vm = pl.BlockSpec(memory_space=pltpu.VMEM)
@@ -346,7 +365,6 @@
             pltpu.SemaphoreType.DMA((3,)),
             pltpu.VMEM((16, width), F32),
             pltpu.VMEM((8, width), jnp.int32),
-            pltpu.VMEM((CB, FB), BF16),
             pltpu.VMEM((EXT, rows), F32),
         ],
         compiler_params=small,

time: 52.5 us -> 43.3 us (0.82)
  starting transfers between devices: 31.6 us -> 16.9 us
  waiting for transfers between devices: 6.64 us -> 13.9 us
  Pallas kernels: 12.6 us -> 10.9 us
    ppermute x10, waiting for transfers between devices: 1.12 us -> 11.7 us  [swap(): return lax.ppermute(values, ('tile', 'wave'), pairs)]
    ppermute x10, starting transfers between devices: 19.6 us -> 10.1 us  [swap(): return lax.ppermute(values, ('tile', 'wave'), pairs)]
    all_to_all x1, starting transfers between devices: 12 us -> 6.75 us  [local(): moms = lax.all_to_all(mom, 'wave', 0, 0)]
    all_to_all x1, waiting for transfers between devices: 5.52 us -> 2.22 us  [local(): moms = lax.all_to_all(mom, 'wave', 0, 0)]
    pallas_call x1, Pallas kernels: 7.92 us -> 6.21 us  [local(): pl.pallas_call(pixel_kernel, in_specs=[sm] + [hb] * 6, out_specs=[vm] * 5...]
  transfers between devices with their start and end apart: 11 -> 11, of which waited for: 5 -> 5; matrix products, arithmetic and copies ran while one was open for 0% -> 0% of each run, Pallas kernels for 15% -> 14%
where the time goes in v2:
time: 43.3 us; the launch traced here: 43.1 us
  starting transfers between devices  16.9 us (39%)
  waiting for transfers between devices  13.9 us (32%)
  Pallas kernels  10.9 us (25%)
  between operations  1.37 us (3%)
    ppermute x10, waiting for transfers between devices, swap(): return lax.ppermute(values, ('tile', 'wave'), pairs)  11.7 us
    ppermute x10, starting transfers between devices, swap(): return lax.ppermute(values, ('tile', 'wave'), pairs)  10.1 us
    all_to_all x1, starting transfers between devices, local(): moms = lax.all_to_all(mom, 'wave', 0, 0)  6.75 us
    pallas_call x1, Pallas kernels, local(): pl.pallas_call(pixel_kernel, in_specs=[sm] + [hb] * 6, out_specs=[vm] * 5...  6.21 us
    all_to_all x1, waiting for transfers between devices, local(): moms = lax.all_to_all(mom, 'wave', 0, 0)  2.22 us
    pallas_call x2, Pallas kernels, local(): pl.pallas_call(functools.partial(next_kernel, step, copies), in_specs=[vm...  2.09 us
    pallas_call x1, Pallas kernels, local(): pl.pallas_call(first_kernel, in_specs=[vm] * 8, out_specs=[vm] * 4, out_s...  0.91 us
  transfers between devices with their start and end apart: 11, of which 5 were waited for; matrix products, arithmetic and copies ran while one was open for 0% of the time, Pallas kernels for 14%

profile of v2, /device:TPU:0, one launch (start us, length us, event | category | flops | bytes accessed | tf_op | source)
XLA Modules:
  0.0 43.1 jit_solution(13806632365957767993)
XLA Ops:
  0.6 0.6 %collective-permute-start = (f32[32,500]{1,0:T(8,128)}, f32[32,500]{1,0:T(8,128)S(1)}, u32[]{:S(2)}, u32[]{:S(2)}) collective-permute-start(f32[32,500]{1,0:T(8,128)} %flux.1), channel_id=1, source_target_pairs={{0,1},{1,0},{2,3},{3,2},{4,5},{5,4},{6,7},{7,6},{8,9},{9,8},{10,11... | collective-permute-start | bytes 192008 | tf_op jit(solution)/shard_map/ppermute | solution.py:329
  1.2 2.6 %collective-permute-start.1 = (f32[32,500]{1,0:T(8,128)}, f32[32,500]{1,0:T(8,128)S(1)}, u32[]{:S(2)}, u32[]{:S(2)}) collective-permute-start(f32[32,500]{1,0:T(8,128)} %flux.1), channel_id=1, source_target_pairs={{0,16},{1,2},{2,1},{3,4},{4,3},{5,6},{6,5},{7,8},{8,7},{9,10},{10,... | collective-permute-start | bytes 192008 | tf_op jit(solution)/shard_map/ppermute | solution.py:329
  4.4 0.0 copy-start
  4.4 6.2 %pixels.1 = (f32[128,512]{1,0:T(8,128)S(1)}, f32[128,512]{1,0:T(8,128)S(1)}, f32[128,512]{1,0:T(8,128)S(1)}, f32[128,64]{1,0:T(8,128)S(1)}, f32[64,128]{1,0:T(8,128)S(1)}) custom-call(s32[1]{0:T(128)S(6)} %copy.10.offsets, s32[1,500]{1,0:T(1,128)} %starts.1, f32[12,1,500]{2,1,0:T(1,128)} %bitcast.3, f32[4,16,32]{2,1,0:T(8,128)} %bitcast.2, ...), custom_call_target="tpu_custom_call" | custom-call | tf_op jit(solution)/shard_map/pixels/pallas_call | solution.py:352
  10.6 0.0 collective-permute-done.flux_e
  10.7 0.0 collective-permute-done.1.flux_o
  10.7 0.0 copy-done
  10.7 0.9 %first.1 = (f32[64,512]{1,0:T(8,128)S(1)}, f32[128,512]{1,0:T(8,128)S(1)}, f32[64,512]{1,0:T(8,128)S(1)}, f32[64,512]{1,0:T(8,128)S(1)}) custom-call(f32[32,500]{1,0:T(8,128)S(1)} %copy-done, f32[32,500]{1,0:T(8,128)S(1)} %collective-permute-done.flux_e, f32[32,500]{1,0:T(8,128)S(1)} %collective-permute-done.1.flux_o, f32[128,512]{1,0:T(8,128)S(1)} %get-tuple-element.29.t0, ...), custom_call_target="tpu_custom_call" | custom-call | tf_op jit(solution)/shard_map/first/pallas_call | solution.py:374
  11.6 0.2 collective-permute-start.2
  11.8 1.5 %collective-permute-start.3 = (f32[64,512]{1,0:T(8,128)S(1)}, f32[64,512]{1,0:T(8,128)S(1)}, u32[]{:S(2)}, u32[]{:S(2)}) collective-permute-start(f32[64,512]{1,0:T(8,128)S(1)} %get-tuple-element.35), channel_id=1, source_target_pairs={{0,16},{1,2},{2,1},{3,4},{4,3},{5,6},{6,5},{7,8},{8,7},{9,10},{10,... | collective-permute-start | bytes 393224 | tf_op jit(solution)/shard_map/ppermute | solution.py:329
  13.3 0.0 collective-permute-done.2.got_e
  13.3 3.4 %collective-permute-done.3.got_o = f32[64,512]{1,0:T(8,128)S(1)} collective-permute-done((f32[64,512]{1,0:T(8,128)S(1)}, f32[64,512]{1,0:T(8,128)S(1)}, u32[]{:S(2)}, u32[]{:S(2)}) %collective-permute-start.3) | collective-permute-done | bytes 131104 | tf_op jit(solution)/shard_map/ppermute | solution.py:329
  16.7 0.8 %second.1 = (f32[64,512]{1,0:T(8,128)S(1)}, f32[64,512]{1,0:T(8,128)S(1)}, f32[8,128]{1,0:T(8,128)S(1)}, f32[64,512]{1,0:T(8,128)S(1)}, f32[32,512]{1,0:T(8,128)S(1)}, /*index=5*/f32[32,512]{1,0:T(8,128)S(1)}) custom-call(f32[128,64]{1,0:T(8,128)S(1)} %get-tuple-element.27.rowmat, f32[64,128]{1,0:T(8,128)S(1)} %get-tuple-element.28.rowmat_t, ...), custom_call_target="tpu_custom_call" | custom-call | tf_op jit(solution)/shard_map/second/pallas_call | solution.py:385
  17.6 0.2 collective-permute-start.4
  17.8 1.5 %collective-permute-start.5 = (f32[32,512]{1,0:T(8,128)S(1)}, f32[32,512]{1,0:T(8,128)S(1)}, u32[]{:S(2)}, u32[]{:S(2)}) collective-permute-start(f32[32,512]{1,0:T(8,128)S(1)} %get-tuple-element.41), channel_id=1, source_target_pairs={{0,16},{1,2},{2,1},{3,4},{4,3},{5,6},{6,5},{7,8},{8,7},{9,10},{10,... | collective-permute-start | bytes 196616 | tf_op jit(solution)/shard_map/ppermute | solution.py:329
  19.2 0.0 collective-permute-done.4.got_e
  19.2 2.8 %collective-permute-done.5.got_o = f32[32,512]{1,0:T(8,128)S(1)} collective-permute-done((f32[32,512]{1,0:T(8,128)S(1)}, f32[32,512]{1,0:T(8,128)S(1)}, u32[]{:S(2)}, u32[]{:S(2)}) %collective-permute-start.5) | collective-permute-done | bytes 65568 | tf_op jit(solution)/shard_map/ppermute | solution.py:329
  22.0 0.8 %next1.1 = (f32[64,512]{1,0:T(8,128)S(1)}, f32[8,128]{1,0:T(8,128)S(1)}, f32[64,512]{1,0:T(8,128)S(1)}, f32[32,512]{1,0:T(8,128)S(1)}, f32[32,512]{1,0:T(8,128)S(1)}) custom-call(f32[128,64]{1,0:T(8,128)S(1)} %get-tuple-element.27.rowmat, f32[64,128]{1,0:T(8,128)S(1)} %get-tuple-element.28.rowmat_t, f32[128,512]{1,0:T(8,128)S(1)} %get-tuple-element.29.t0, ...), custom_call_target="tpu_custom_call" | custom-call | tf_op jit(solution)/shard_map/next1/pallas_call | solution.py:398
  22.9 0.2 collective-permute-start.6
  23.1 1.5 %collective-permute-start.7 = (f32[32,512]{1,0:T(8,128)S(1)}, f32[32,512]{1,0:T(8,128)S(1)}, u32[]{:S(2)}, u32[]{:S(2)}) collective-permute-start(f32[32,512]{1,0:T(8,128)S(1)} %get-tuple-element.46), channel_id=1, source_target_pairs={{0,16},{1,2},{2,1},{3,4},{4,3},{5,6},{6,5},{7,8},{8,7},{9,10},{10,... | collective-permute-start | bytes 196616 | tf_op jit(solution)/shard_map/ppermute | solution.py:329
  24.6 0.0 collective-permute-done.6.got_e
  24.6 2.7 %collective-permute-done.7.got_o = f32[32,512]{1,0:T(8,128)S(1)} collective-permute-done((f32[32,512]{1,0:T(8,128)S(1)}, f32[32,512]{1,0:T(8,128)S(1)}, u32[]{:S(2)}, u32[]{:S(2)}) %collective-permute-start.7) | collective-permute-done | bytes 65568 | tf_op jit(solution)/shard_map/ppermute | solution.py:329
  27.4 1.2 %next2.1 = (f32[64,512]{1,0:T(8,128)S(1)}, f32[16,8,128]{2,1,0:T(8,128)}, f32[64,512]{1,0:T(8,128)S(1)}, f32[32,512]{1,0:T(8,128)S(1)}, f32[32,512]{1,0:T(8,128)S(1)}) custom-call(f32[128,64]{1,0:T(8,128)S(1)} %get-tuple-element.27.rowmat, f32[64,128]{1,0:T(8,128)S(1)} %get-tuple-element.28.rowmat_t, f32[128,512]{1,0:T(8,128)S(1)} %get-tuple-element.29.t0, ...), custom_call_target="tpu_custom_call" | custom-call | tf_op jit(solution)/shard_map/next2/pallas_call | solution.py:398
  28.6 6.8 %all-to-all-start = ((f32[16,8,128]{2,1,0:T(8,128)}), f32[16,8,128]{2,1,0:T(8,128)S(1)}, u32[]{:S(2)}, u32[]{:S(2)}) async-start(f32[16,8,128]{2,1,0:T(8,128)} %get-tuple-element.47), calls=%async_computation | async-start | bytes 131072 | tf_op jit(solution)/shard_map/all_to_all | solution.py:408
  35.4 0.4 collective-permute-start.8
  35.8 1.5 %collective-permute-start.9 = (f32[32,512]{1,0:T(8,128)S(1)}, f32[32,512]{1,0:T(8,128)S(1)}, u32[]{:S(2)}, u32[]{:S(2)}) collective-permute-start(f32[32,512]{1,0:T(8,128)S(1)} %get-tuple-element.51), channel_id=1, source_target_pairs={{0,16},{1,2},{2,1},{3,4},{4,3},{5,6},{6,5},{7,8},{8,7},{9,10},{10,... | collective-permute-start | bytes 196616 | tf_op jit(solution)/shard_map/ppermute | solution.py:329
  37.3 0.0 collective-permute-done.8.got_e
  37.3 2.7 %collective-permute-done.9.got_o = f32[32,512]{1,0:T(8,128)S(1)} collective-permute-done((f32[32,512]{1,0:T(8,128)S(1)}, f32[32,512]{1,0:T(8,128)S(1)}, u32[]{:S(2)}, u32[]{:S(2)}) %collective-permute-start.9) | collective-permute-done | bytes 65568 | tf_op jit(solution)/shard_map/ppermute | solution.py:329
  40.0 2.2 %all-to-all-done.moms = f32[16,8,128]{2,1,0:T(8,128)S(1)} async-done(((f32[16,8,128]{2,1,0:T(8,128)}), f32[16,8,128]{2,1,0:T(8,128)S(1)}, u32[]{:S(2)}, u32[]{:S(2)}) %all-to-all-start) | async-done | bytes 65568 | tf_op jit(solution)/shard_map/all_to_all | solution.py:408
  42.3 0.8 %last.1 = (f32[32,500]{1,0:T(8,128)}, f32[32,500]{1,0:T(8,128)}) custom-call(f32[16,8,128]{2,1,0:T(8,128)S(1)} %all-to-all-done.moms, f32[64,512]{1,0:T(8,128)S(1)} %get-tuple-element.36.diag, f32[64,512]{1,0:T(8,128)S(1)} %get-tuple-element.32.start_ext, f32[64,512]{1,0:T(8,128)S(1)} %get-tuple-element.37.before.p0, ...), custom_call_target="tpu_custom_call" | custom-call | tf_op jit(solution)/shard_map/last/pallas_call | solution.py:410
Async XLA Ops:
  0.6 10.0 %collective-permute-start = (f32[32,500]{1,0:T(8,128)}, f32[32,500]{1,0:T(8,128)S(1)}, u32[]{:S(2)}, u32[]{:S(2)}) collective-permute-start(f32[32,500]{1,0:T(8,128)} %flux.1), channel_id=1, source_target_pairs={{0,1},{1,0},{2,3},{3,2},{4,5},{5,4},{6,7},{7,6},{8,9},{9,8},{10,11... | collective-permute-start | bytes 192008 | tf_op jit(solution)/shard_map/ppermute | solution.py:329
  1.2 9.5 %collective-permute-start.1 = (f32[32,500]{1,0:T(8,128)}, f32[32,500]{1,0:T(8,128)S(1)}, u32[]{:S(2)}, u32[]{:S(2)}) collective-permute-start(f32[32,500]{1,0:T(8,128)} %flux.1), channel_id=1, source_target_pairs={{0,16},{1,2},{2,1},{3,4},{4,3},{5,6},{6,5},{7,8},{8,7},{9,10},{10,... | collective-permute-start | bytes 192008 | tf_op jit(solution)/shard_map/ppermute | solution.py:329
  4.4 6.2 %copy-start = (f32[32,500]{1,0:T(8,128)S(1)}, f32[32,500]{1,0:T(8,128)}, u32[]{:S(2)}) copy-start(f32[32,500]{1,0:T(8,128)} %flux.1) | copy-start | bytes 192004
  11.6 1.7 %collective-permute-start.2 = (f32[64,512]{1,0:T(8,128)S(1)}, f32[64,512]{1,0:T(8,128)S(1)}, u32[]{:S(2)}, u32[]{:S(2)}) collective-permute-start(f32[64,512]{1,0:T(8,128)S(1)} %get-tuple-element.34), channel_id=1, source_target_pairs={{0,1},{1,0},{2,3},{3,2},{4,5},{5,4},{6,7},{7,6},{8,9},{9,8},{10,11... | collective-permute-start | bytes 393224 | tf_op jit(solution)/shard_map/ppermute | solution.py:329
  11.8 5.0 %collective-permute-start.3 = (f32[64,512]{1,0:T(8,128)S(1)}, f32[64,512]{1,0:T(8,128)S(1)}, u32[]{:S(2)}, u32[]{:S(2)}) collective-permute-start(f32[64,512]{1,0:T(8,128)S(1)} %get-tuple-element.35), channel_id=1, source_target_pairs={{0,16},{1,2},{2,1},{3,4},{4,3},{5,6},{6,5},{7,8},{8,7},{9,10},{10,... | collective-permute-start | bytes 393224 | tf_op jit(solution)/shard_map/ppermute | solution.py:329
  17.6 1.7 %collective-permute-start.4 = (f32[32,512]{1,0:T(8,128)S(1)}, f32[32,512]{1,0:T(8,128)S(1)}, u32[]{:S(2)}, u32[]{:S(2)}) collective-permute-start(f32[32,512]{1,0:T(8,128)S(1)} %get-tuple-element.40), channel_id=1, source_target_pairs={{0,1},{1,0},{2,3},{3,2},{4,5},{5,4},{6,7},{7,6},{8,9},{9,8},{10,11... | collective-permute-start | bytes 196616 | tf_op jit(solution)/shard_map/ppermute | solution.py:329
  17.8 4.3 %collective-permute-start.5 = (f32[32,512]{1,0:T(8,128)S(1)}, f32[32,512]{1,0:T(8,128)S(1)}, u32[]{:S(2)}, u32[]{:S(2)}) collective-permute-start(f32[32,512]{1,0:T(8,128)S(1)} %get-tuple-element.41), channel_id=1, source_target_pairs={{0,16},{1,2},{2,1},{3,4},{4,3},{5,6},{6,5},{7,8},{8,7},{9,10},{10,... | collective-permute-start | bytes 196616 | tf_op jit(solution)/shard_map/ppermute | solution.py:329
  22.9 1.7 %collective-permute-start.6 = (f32[32,512]{1,0:T(8,128)S(1)}, f32[32,512]{1,0:T(8,128)S(1)}, u32[]{:S(2)}, u32[]{:S(2)}) collective-permute-start(f32[32,512]{1,0:T(8,128)S(1)} %get-tuple-element.45), channel_id=1, source_target_pairs={{0,1},{1,0},{2,3},{3,2},{4,5},{5,4},{6,7},{7,6},{8,9},{9,8},{10,11... | collective-permute-start | bytes 196616 | tf_op jit(solution)/shard_map/ppermute | solution.py:329
  23.1 4.3 %collective-permute-start.7 = (f32[32,512]{1,0:T(8,128)S(1)}, f32[32,512]{1,0:T(8,128)S(1)}, u32[]{:S(2)}, u32[]{:S(2)}) collective-permute-start(f32[32,512]{1,0:T(8,128)S(1)} %get-tuple-element.46), channel_id=1, source_target_pairs={{0,16},{1,2},{2,1},{3,4},{4,3},{5,6},{6,5},{7,8},{8,7},{9,10},{10,... | collective-permute-start | bytes 196616 | tf_op jit(solution)/shard_map/ppermute | solution.py:329
  28.6 13.7 %all-to-all-start = ((f32[16,8,128]{2,1,0:T(8,128)}), f32[16,8,128]{2,1,0:T(8,128)S(1)}, u32[]{:S(2)}, u32[]{:S(2)}) async-start(f32[16,8,128]{2,1,0:T(8,128)} %get-tuple-element.47), calls=%async_computation | async-start | bytes 131072 | tf_op jit(solution)/shard_map/all_to_all | solution.py:408
  35.4 1.9 %collective-permute-start.8 = (f32[32,512]{1,0:T(8,128)S(1)}, f32[32,512]{1,0:T(8,128)S(1)}, u32[]{:S(2)}, u32[]{:S(2)}) collective-permute-start(f32[32,512]{1,0:T(8,128)S(1)} %get-tuple-element.50), channel_id=1, source_target_pairs={{0,1},{1,0},{2,3},{3,2},{4,5},{5,4},{6,7},{7,6},{8,9},{9,8},{10,11... | collective-permute-start | bytes 196616 | tf_op jit(solution)/shard_map/ppermute | solution.py:329
  35.8 4.3 %collective-permute-start.9 = (f32[32,512]{1,0:T(8,128)S(1)}, f32[32,512]{1,0:T(8,128)S(1)}, u32[]{:S(2)}, u32[]{:S(2)}) collective-permute-start(f32[32,512]{1,0:T(8,128)S(1)} %get-tuple-element.51), channel_id=1, source_target_pairs={{0,16},{1,2},{2,1},{3,4},{4,3},{5,6},{6,5},{7,8},{8,7},{9,10},{10,... | collective-permute-start | bytes 196616 | tf_op jit(solution)/shard_map/ppermute | solution.py:329

commit v3 on v2

--- a/solution.py
+++ b/solution.py
@@ -6,6 +6,7 @@
 from jax.experimental import pallas as pl
 from jax.experimental.pallas import tpu as pltpu
 from jax.sharding import PartitionSpec as P
+
 
 SLAB_ROWS = 32
 HALO = 32
@@ -20,7 +21,7 @@
 FB = 128
 CB = FB * PITCH
 VMEM_LIMIT = 16 * 1024 * 1024
-SHIFT = 10.0
+SHIFT = 14.0
 PRECISE = lax.Precision.HIGHEST
 F32 = jnp.float32
 BF16 = jnp.bfloat16
@@ -71,7 +72,7 @@
             pltpu.make_async_copy(src.at[:, :, cols], dst.at[:, :, cols], sems.at[b, i])
             for i, (src, dst) in enumerate(((inverse_var, inv_s), (masked, mask_s), (frames, frames_s)))
         ])
-    for c in copies[0]:
+    for c in copies[0] + copies[1]:
         c.start()
 
     pad_s[...] = jnp.zeros_like(pad_s)
@@ -81,7 +82,7 @@
         c.wait()
     for i in range(rows // SLAB_ROWS):
         band_s[0:BAND, i * SLAB_ROWS : (i + 1) * SLAB_ROWS] = bands_s[i]
-    for c in copies[1]:
+    for c in copies[2] + copies[3]:
         c.start()
     rt = row_matrix(band_s[...], offsets[0])
     rowmat_t[...] = rt
@@ -136,11 +137,9 @@
         return t[:, 0:FB], t[:, FB:], g
 
     for b in range(blocks):
-        for c in copies[b]:
-            c.wait()
-        if b + 2 < blocks:
-            for c in copies[b + 2]:
-                c.start()
+        if b % 2 == 0:
+            for c in copies[b] + copies[b + 1]:
+                c.wait()
         at = slice(b * CB, (b + 1) * CB)
         w = (inv_s[:, :, at] * (1.0 - mask_s[:, :, at].astype(F32))).reshape(rows, CB)
         v = w * frames_s[:, :, at].reshape(rows, CB)
@@ -248,8 +247,14 @@
     vec[...] = p
     scaled = own(d) * own(p)
     u, t, back = apply_rows(p, rowmat, rowmat_t, t0, t1)
-    part_out[...] = back
-    split(back, parity, send_e, send_o, 0)
+    if copies:
+        part_out[...] = own(back)
+        low, high = back[0:GHOST], back[EXT - GHOST : EXT]
+        send_e[...] = jnp.where(parity == 0, high, low)
+        send_o[...] = jnp.where(parity == 0, low, high)
+    else:
+        part_out[...] = back
+        split(back, parity, send_e, send_o, 0)
     moments = mom[...]
     row = lax.broadcasted_iota(jnp.int32, moments.shape, 0)
     new = [(2 * step - 1, lanes_of(scaled * own(prev))), (2 * step, lanes_of(scaled * own(p)))]
@@ -305,7 +310,9 @@
     chi = [wide(c) for c in chi]
     rho = [wide(c) for c in rho]
     q0, q1, q2, d = own(p0), own(p1), own(p2), own(diag)
-    image = own(joined(part, got_e, got_o, 0)) + RIDGE * q2
+    low, high = sides(got_e[...], got_o[...])
+    between = jnp.zeros((SLAB_ROWS - 2 * GHOST, width), F32)
+    image = part[...] + jnp.concatenate([low, between, high] if SLAB_ROWS > 2 * GHOST else [low, high], 0) + RIDGE * q2
     x = own(start_ext) + chi[0] * q0 + chi[1] * q1 + chi[2] * q2
     r = d * (rho[0] * q0 + rho[1] * q1 + rho[2] * q2) + rho[3] * (image - SHIFT * (d * q2))
     solution_ref[...] = x[:, 0:fib]
@@ -325,8 +332,10 @@
     return even, odd
 
 
-def swap(values, pairs):
-    return lax.ppermute(values, ("tile", "wave"), pairs)
+def swap(send_o, odd, send_e, even):
+    got_o = lax.ppermute(send_o, ("tile", "wave"), odd)
+    got_e = lax.ppermute(send_e, ("tile", "wave"), even)
+    return got_o, got_e
 
 
 def local(frames, inverse_var, masked, psf_band, offsets, starts, profile, flux_start):
@@ -337,7 +346,7 @@
     blocks = columns // CB
     width = blocks * FB
     even, odd = partners(lax.axis_size("tile"), waves)
-    flux_o, flux_e = swap(flux_start, odd), swap(flux_start, even)
+    flux_o, flux_e = swap(flux_start, odd, flux_start, even)
 
     vm = pl.BlockSpec(memory_space=pltpu.VMEM)
     small = pltpu.CompilerParams(vmem_limit_bytes=VMEM_LIMIT)
@@ -380,7 +389,7 @@
         compiler_params=small,
         name="first",
     )(flux_start, flux_e, flux_o, t0, t1, f, rowmat, rowmat_t)
-    got_o, got_e = swap(send_o, odd), swap(send_e, even)
+    got_o, got_e = swap(send_o, odd, send_e, even)
 
     diag, p0, mom, part, send_e, send_o = pl.pallas_call(
         second_kernel,
@@ -392,19 +401,18 @@
     )(rowmat, rowmat_t, t0, t1, start_ext, part, got_e, got_o)
     vectors = [p0]
     for step in (1, 2):
-        got_o, got_e = swap(send_o, odd), swap(send_e, even)
+        got_o, got_e = swap(send_o, odd, send_e, even)
         copies = waves if step == 2 else 0
         mom_shape = shape(waves, 8, LANES) if copies else shape(8, LANES)
         vec, mom, part, send_e, send_o = pl.pallas_call(
             functools.partial(next_kernel, step, copies),
             in_specs=[vm] * 10,
             out_specs=[vm] * 5,
-            out_shape=[shape(EXT, width), mom_shape, shape(EXT, width), shape(HALF, width), shape(HALF, width)],
+            out_shape=[shape(EXT, width), mom_shape, shape(EXT if step == 1 else slab, width), *[shape(HALF if step == 1 else GHOST, width)] * 2],
             compiler_params=small,
-            name=f"next{step}",
         )(rowmat, rowmat_t, t0, t1, diag, vectors[-1], mom, part, got_e, got_o)
         vectors.append(vec)
-    got_o, got_e = swap(send_o, odd), swap(send_e, even)
+    got_o, got_e = swap(send_o, odd, send_e, even)
     moms = lax.all_to_all(mom, "wave", 0, 0)
     return tuple(
         pl.pallas_call(

time: 43.3 us -> 42.9 us (level)
  no operation moved by 1% of the time
where the time goes in v3:
time: 42.9 us; the launch traced here: 42.7 us
  starting transfers between devices  16.9 us (39%)
  waiting for transfers between devices  14 us (33%)
  Pallas kernels  10.5 us (24%)
  between operations  1.37 us (3%)
    ppermute x5, waiting for transfers between devices, swap(): got_o = lax.ppermute(send_o, ('tile', 'wave'), odd)  11.4 us
    ppermute x5, starting transfers between devices, swap(): got_o = lax.ppermute(send_o, ('tile', 'wave'), odd)  8.61 us
    all_to_all x1, starting transfers between devices, local(): moms = lax.all_to_all(mom, 'wave', 0, 0)  6.75 us
    pallas_call x1, Pallas kernels, local(): pl.pallas_call(pixel_kernel, in_specs=[sm] + [hb] * 6, out_specs=[vm] * 5...  5.78 us
    all_to_all x1, waiting for transfers between devices, local(): moms = lax.all_to_all(mom, 'wave', 0, 0)  2.57 us
    pallas_call x2, Pallas kernels, local(): pl.pallas_call(functools.partial(next_kernel, step, copies), in_specs=[vm...  2.08 us
    ppermute x5, starting transfers between devices, swap(): got_e = lax.ppermute(send_e, ('tile', 'wave'), even)  1.53 us
    pallas_call x1, Pallas kernels, local(): pl.pallas_call(first_kernel, in_specs=[vm] * 8, out_specs=[vm] * 4, out_s...  0.91 us
  transfers between devices with their start and end apart: 11, of which 5 were waited for; matrix products, arithmetic and copies ran while one was open for 0% of the time, Pallas kernels for 14%

profile of v3, /device:TPU:0, one launch (start us, length us, event | category | flops | bytes accessed | tf_op | source)
XLA Modules:
  0.0 42.7 jit_solution(17250298242061699888)
XLA Ops:
  0.6 0.6 %collective-permute-start = (f32[32,500]{1,0:T(8,128)}, f32[32,500]{1,0:T(8,128)S(1)}, u32[]{:S(2)}, u32[]{:S(2)}) collective-permute-start(f32[32,500]{1,0:T(8,128)} %flux.1), channel_id=1, source_target_pairs={{0,1},{1,0},{2,3},{3,2},{4,5},{5,4},{6,7},{7,6},{8,9},{9,8},{10,11... | collective-permute-start | bytes 192008 | tf_op jit(solution)/shard_map/ppermute | solution.py:337
  1.2 2.6 %collective-permute-start.1 = (f32[32,500]{1,0:T(8,128)}, f32[32,500]{1,0:T(8,128)S(1)}, u32[]{:S(2)}, u32[]{:S(2)}) collective-permute-start(f32[32,500]{1,0:T(8,128)} %flux.1), channel_id=1, source_target_pairs={{0,16},{1,2},{2,1},{3,4},{4,3},{5,6},{6,5},{7,8},{8,7},{9,10},{10,... | collective-permute-start | bytes 192008 | tf_op jit(solution)/shard_map/ppermute | solution.py:336
  4.4 0.0 copy-start
  4.4 5.8 %pixels.1 = (f32[128,512]{1,0:T(8,128)S(1)}, f32[128,512]{1,0:T(8,128)S(1)}, f32[128,512]{1,0:T(8,128)S(1)}, f32[128,64]{1,0:T(8,128)S(1)}, f32[64,128]{1,0:T(8,128)S(1)}) custom-call(s32[1]{0:T(128)S(6)} %copy.10.offsets, s32[1,500]{1,0:T(1,128)} %starts.1, f32[12,1,500]{2,1,0:T(1,128)} %bitcast.3, f32[4,16,32]{2,1,0:T(8,128)} %bitcast.2, ...), custom_call_target="tpu_custom_call" | custom-call | tf_op jit(solution)/shard_map/pixels/pallas_call | solution.py:361
  10.2 0.0 collective-permute-done.flux_e
  10.2 0.0 collective-permute-done.1.flux_o
  10.2 0.0 copy-done
  10.3 0.9 %first.1 = (f32[64,512]{1,0:T(8,128)S(1)}, f32[128,512]{1,0:T(8,128)S(1)}, f32[64,512]{1,0:T(8,128)S(1)}, f32[64,512]{1,0:T(8,128)S(1)}) custom-call(f32[32,500]{1,0:T(8,128)S(1)} %copy-done, f32[32,500]{1,0:T(8,128)S(1)} %collective-permute-done.flux_e, f32[32,500]{1,0:T(8,128)S(1)} %collective-permute-done.1.flux_o, f32[128,512]{1,0:T(8,128)S(1)} %get-tuple-element.29.t0, ...), custom_call_target="tpu_custom_call" | custom-call | tf_op jit(solution)/shard_map/first/pallas_call | solution.py:383
  11.2 0.2 collective-permute-start.2
  11.3 1.5 %collective-permute-start.3 = (f32[64,512]{1,0:T(8,128)S(1)}, f32[64,512]{1,0:T(8,128)S(1)}, u32[]{:S(2)}, u32[]{:S(2)}) collective-permute-start(f32[64,512]{1,0:T(8,128)S(1)} %get-tuple-element.35), channel_id=1, source_target_pairs={{0,16},{1,2},{2,1},{3,4},{4,3},{5,6},{6,5},{7,8},{8,7},{9,10},{10,... | collective-permute-start | bytes 393224 | tf_op jit(solution)/shard_map/ppermute | solution.py:336
  12.9 0.0 collective-permute-done.2.got_e
  12.9 3.4 %collective-permute-done.3.got_o = f32[64,512]{1,0:T(8,128)S(1)} collective-permute-done((f32[64,512]{1,0:T(8,128)S(1)}, f32[64,512]{1,0:T(8,128)S(1)}, u32[]{:S(2)}, u32[]{:S(2)}) %collective-permute-start.3) | collective-permute-done | bytes 131104 | tf_op jit(solution)/shard_map/ppermute | solution.py:336
  16.3 0.8 %second.1 = (f32[64,512]{1,0:T(8,128)S(1)}, f32[64,512]{1,0:T(8,128)S(1)}, f32[8,128]{1,0:T(8,128)S(1)}, f32[64,512]{1,0:T(8,128)S(1)}, f32[32,512]{1,0:T(8,128)S(1)}, /*index=5*/f32[32,512]{1,0:T(8,128)S(1)}) custom-call(f32[128,64]{1,0:T(8,128)S(1)} %get-tuple-element.27.rowmat, f32[64,128]{1,0:T(8,128)S(1)} %get-tuple-element.28.rowmat_t, ...), custom_call_target="tpu_custom_call" | custom-call | tf_op jit(solution)/shard_map/second/pallas_call | solution.py:394
  17.2 0.2 collective-permute-start.4
  17.3 1.5 %collective-permute-start.5 = (f32[32,512]{1,0:T(8,128)S(1)}, f32[32,512]{1,0:T(8,128)S(1)}, u32[]{:S(2)}, u32[]{:S(2)}) collective-permute-start(f32[32,512]{1,0:T(8,128)S(1)} %get-tuple-element.41), channel_id=1, source_target_pairs={{0,16},{1,2},{2,1},{3,4},{4,3},{5,6},{6,5},{7,8},{8,7},{9,10},{10,... | collective-permute-start | bytes 196616 | tf_op jit(solution)/shard_map/ppermute | solution.py:336
  18.8 0.0 collective-permute-done.4.got_e
  18.8 2.8 %collective-permute-done.5.got_o = f32[32,512]{1,0:T(8,128)S(1)} collective-permute-done((f32[32,512]{1,0:T(8,128)S(1)}, f32[32,512]{1,0:T(8,128)S(1)}, u32[]{:S(2)}, u32[]{:S(2)}) %collective-permute-start.5) | collective-permute-done | bytes 65568 | tf_op jit(solution)/shard_map/ppermute | solution.py:336
  21.6 0.8 %shard_map.95 = (f32[64,512]{1,0:T(8,128)S(1)}, f32[8,128]{1,0:T(8,128)S(1)}, f32[64,512]{1,0:T(8,128)S(1)}, f32[32,512]{1,0:T(8,128)S(1)}, f32[32,512]{1,0:T(8,128)S(1)}) custom-call(f32[128,64]{1,0:T(8,128)S(1)} %get-tuple-element.27.rowmat, f32[64,128]{1,0:T(8,128)S(1)} %get-tuple-element.28.rowmat_t, f32[128,512]{1,0:T(8,128)S(1)} %get-tuple-element.29.t0, ...), custom_call_target="tpu_custom_call" | custom-call | tf_op jit(solution)/shard_map/pallas_call | solution.py:407
  22.5 0.2 collective-permute-start.6
  22.7 1.5 %collective-permute-start.7 = (f32[32,512]{1,0:T(8,128)S(1)}, f32[32,512]{1,0:T(8,128)S(1)}, u32[]{:S(2)}, u32[]{:S(2)}) collective-permute-start(f32[32,512]{1,0:T(8,128)S(1)} %get-tuple-element.46), channel_id=1, source_target_pairs={{0,16},{1,2},{2,1},{3,4},{4,3},{5,6},{6,5},{7,8},{8,7},{9,10},{10,... | collective-permute-start | bytes 196616 | tf_op jit(solution)/shard_map/ppermute | solution.py:336
  24.2 0.0 collective-permute-done.6.got_e
  24.2 2.8 %collective-permute-done.7.got_o = f32[32,512]{1,0:T(8,128)S(1)} collective-permute-done((f32[32,512]{1,0:T(8,128)S(1)}, f32[32,512]{1,0:T(8,128)S(1)}, u32[]{:S(2)}, u32[]{:S(2)}) %collective-permute-start.7) | collective-permute-done | bytes 65568 | tf_op jit(solution)/shard_map/ppermute | solution.py:336
  26.9 1.2 %shard_map.96 = (f32[64,512]{1,0:T(8,128)S(1)}, f32[16,8,128]{2,1,0:T(8,128)}, f32[32,512]{1,0:T(8,128)S(1)}, f32[16,512]{1,0:T(8,128)S(1)}, f32[16,512]{1,0:T(8,128)S(1)}) custom-call(f32[128,64]{1,0:T(8,128)S(1)} %get-tuple-element.27.rowmat, f32[64,128]{1,0:T(8,128)S(1)} %get-tuple-element.28.rowmat_t, f32[128,512]{1,0:T(8,128)S(1)} %get-tuple-element.29.t0, ...), custom_call_target="tpu_custom_call" | custom-call | tf_op jit(solution)/shard_map/pallas_call | solution.py:407
  28.2 6.7 %all-to-all-start = ((f32[16,8,128]{2,1,0:T(8,128)}), f32[16,8,128]{2,1,0:T(8,128)S(1)}, u32[]{:S(2)}, u32[]{:S(2)}) async-start(f32[16,8,128]{2,1,0:T(8,128)} %get-tuple-element.47), calls=%async_computation | async-start | bytes 131072 | tf_op jit(solution)/shard_map/all_to_all | solution.py:416
  34.9 0.4 collective-permute-start.8
  35.3 1.5 %collective-permute-start.9 = (f32[16,512]{1,0:T(8,128)S(1)}, f32[16,512]{1,0:T(8,128)S(1)}, u32[]{:S(2)}, u32[]{:S(2)}) collective-permute-start(f32[16,512]{1,0:T(8,128)S(1)} %get-tuple-element.51), channel_id=1, source_target_pairs={{0,16},{1,2},{2,1},{3,4},{4,3},{5,6},{6,5},{7,8},{8,7},{9,10},{10,... | collective-permute-start | bytes 98312 | tf_op jit(solution)/shard_map/ppermute | solution.py:336
  36.9 0.0 collective-permute-done.8.got_e
  36.9 2.4 %collective-permute-done.9.got_o = f32[16,512]{1,0:T(8,128)S(1)} collective-permute-done((f32[16,512]{1,0:T(8,128)S(1)}, f32[16,512]{1,0:T(8,128)S(1)}, u32[]{:S(2)}, u32[]{:S(2)}) %collective-permute-start.9) | collective-permute-done | bytes 32800 | tf_op jit(solution)/shard_map/ppermute | solution.py:336
  39.3 2.6 %all-to-all-done.moms = f32[16,8,128]{2,1,0:T(8,128)S(1)} async-done(((f32[16,8,128]{2,1,0:T(8,128)}), f32[16,8,128]{2,1,0:T(8,128)S(1)}, u32[]{:S(2)}, u32[]{:S(2)}) %all-to-all-start) | async-done | bytes 65568 | tf_op jit(solution)/shard_map/all_to_all | solution.py:416
  41.8 0.8 %last.1 = (f32[32,500]{1,0:T(8,128)}, f32[32,500]{1,0:T(8,128)}) custom-call(f32[16,8,128]{2,1,0:T(8,128)S(1)} %all-to-all-done.moms, f32[64,512]{1,0:T(8,128)S(1)} %get-tuple-element.36.diag, f32[64,512]{1,0:T(8,128)S(1)} %get-tuple-element.32.start_ext, f32[64,512]{1,0:T(8,128)S(1)} %get-tuple-element.37.before.p0, ...), custom_call_target="tpu_custom_call" | custom-call | tf_op jit(solution)/shard_map/last/pallas_call | solution.py:418
Async XLA Ops:
  0.6 9.6 %collective-permute-start = (f32[32,500]{1,0:T(8,128)}, f32[32,500]{1,0:T(8,128)S(1)}, u32[]{:S(2)}, u32[]{:S(2)}) collective-permute-start(f32[32,500]{1,0:T(8,128)} %flux.1), channel_id=1, source_target_pairs={{0,1},{1,0},{2,3},{3,2},{4,5},{5,4},{6,7},{7,6},{8,9},{9,8},{10,11... | collective-permute-start | bytes 192008 | tf_op jit(solution)/shard_map/ppermute | solution.py:337
  1.2 9.0 %collective-permute-start.1 = (f32[32,500]{1,0:T(8,128)}, f32[32,500]{1,0:T(8,128)S(1)}, u32[]{:S(2)}, u32[]{:S(2)}) collective-permute-start(f32[32,500]{1,0:T(8,128)} %flux.1), channel_id=1, source_target_pairs={{0,16},{1,2},{2,1},{3,4},{4,3},{5,6},{6,5},{7,8},{8,7},{9,10},{10,... | collective-permute-start | bytes 192008 | tf_op jit(solution)/shard_map/ppermute | solution.py:336
  4.4 5.8 %copy-start = (f32[32,500]{1,0:T(8,128)S(1)}, f32[32,500]{1,0:T(8,128)}, u32[]{:S(2)}) copy-start(f32[32,500]{1,0:T(8,128)} %flux.1) | copy-start | bytes 192004
  11.2 1.7 %collective-permute-start.2 = (f32[64,512]{1,0:T(8,128)S(1)}, f32[64,512]{1,0:T(8,128)S(1)}, u32[]{:S(2)}, u32[]{:S(2)}) collective-permute-start(f32[64,512]{1,0:T(8,128)S(1)} %get-tuple-element.34), channel_id=1, source_target_pairs={{0,1},{1,0},{2,3},{3,2},{4,5},{5,4},{6,7},{7,6},{8,9},{9,8},{10,11... | collective-permute-start | bytes 393224 | tf_op jit(solution)/shard_map/ppermute | solution.py:337
  11.3 5.0 %collective-permute-start.3 = (f32[64,512]{1,0:T(8,128)S(1)}, f32[64,512]{1,0:T(8,128)S(1)}, u32[]{:S(2)}, u32[]{:S(2)}) collective-permute-start(f32[64,512]{1,0:T(8,128)S(1)} %get-tuple-element.35), channel_id=1, source_target_pairs={{0,16},{1,2},{2,1},{3,4},{4,3},{5,6},{6,5},{7,8},{8,7},{9,10},{10,... | collective-permute-start | bytes 393224 | tf_op jit(solution)/shard_map/ppermute | solution.py:336
  17.2 1.7 %collective-permute-start.4 = (f32[32,512]{1,0:T(8,128)S(1)}, f32[32,512]{1,0:T(8,128)S(1)}, u32[]{:S(2)}, u32[]{:S(2)}) collective-permute-start(f32[32,512]{1,0:T(8,128)S(1)} %get-tuple-element.40), channel_id=1, source_target_pairs={{0,1},{1,0},{2,3},{3,2},{4,5},{5,4},{6,7},{7,6},{8,9},{9,8},{10,11... | collective-permute-start | bytes 196616 | tf_op jit(solution)/shard_map/ppermute | solution.py:337
  17.3 4.3 %collective-permute-start.5 = (f32[32,512]{1,0:T(8,128)S(1)}, f32[32,512]{1,0:T(8,128)S(1)}, u32[]{:S(2)}, u32[]{:S(2)}) collective-permute-start(f32[32,512]{1,0:T(8,128)S(1)} %get-tuple-element.41), channel_id=1, source_target_pairs={{0,16},{1,2},{2,1},{3,4},{4,3},{5,6},{6,5},{7,8},{8,7},{9,10},{10,... | collective-permute-start | bytes 196616 | tf_op jit(solution)/shard_map/ppermute | solution.py:336
  22.5 1.7 %collective-permute-start.6 = (f32[32,512]{1,0:T(8,128)S(1)}, f32[32,512]{1,0:T(8,128)S(1)}, u32[]{:S(2)}, u32[]{:S(2)}) collective-permute-start(f32[32,512]{1,0:T(8,128)S(1)} %get-tuple-element.45), channel_id=1, source_target_pairs={{0,1},{1,0},{2,3},{3,2},{4,5},{5,4},{6,7},{7,6},{8,9},{9,8},{10,11... | collective-permute-start | bytes 196616 | tf_op jit(solution)/shard_map/ppermute | solution.py:337
  22.7 4.3 %collective-permute-start.7 = (f32[32,512]{1,0:T(8,128)S(1)}, f32[32,512]{1,0:T(8,128)S(1)}, u32[]{:S(2)}, u32[]{:S(2)}) collective-permute-start(f32[32,512]{1,0:T(8,128)S(1)} %get-tuple-element.46), channel_id=1, source_target_pairs={{0,16},{1,2},{2,1},{3,4},{4,3},{5,6},{6,5},{7,8},{8,7},{9,10},{10,... | collective-permute-start | bytes 196616 | tf_op jit(solution)/shard_map/ppermute | solution.py:336
  28.2 13.7 %all-to-all-start = ((f32[16,8,128]{2,1,0:T(8,128)}), f32[16,8,128]{2,1,0:T(8,128)S(1)}, u32[]{:S(2)}, u32[]{:S(2)}) async-start(f32[16,8,128]{2,1,0:T(8,128)} %get-tuple-element.47), calls=%async_computation | async-start | bytes 131072 | tf_op jit(solution)/shard_map/all_to_all | solution.py:416
  34.9 1.9 %collective-permute-start.8 = (f32[16,512]{1,0:T(8,128)S(1)}, f32[16,512]{1,0:T(8,128)S(1)}, u32[]{:S(2)}, u32[]{:S(2)}) collective-permute-start(f32[16,512]{1,0:T(8,128)S(1)} %get-tuple-element.50), channel_id=1, source_target_pairs={{0,1},{1,0},{2,3},{3,2},{4,5},{5,4},{6,7},{7,6},{8,9},{9,8},{10,11... | collective-permute-start | bytes 98312 | tf_op jit(solution)/shard_map/ppermute | solution.py:337
  35.3 3.9 %collective-permute-start.9 = (f32[16,512]{1,0:T(8,128)S(1)}, f32[16,512]{1,0:T(8,128)S(1)}, u32[]{:S(2)}, u32[]{:S(2)}) collective-permute-start(f32[16,512]{1,0:T(8,128)S(1)} %get-tuple-element.51), channel_id=1, source_target_pairs={{0,16},{1,2},{2,1},{3,4},{4,3},{5,6},{6,5},{7,8},{8,7},{9,10},{10,... | collective-permute-start | bytes 98312 | tf_op jit(solution)/shard_map/ppermute | solution.py:336

commit v4 on v3

--- a/solution.py
+++ b/solution.py
@@ -1,5 +1,3 @@
-import functools
-
 import jax
 import jax.numpy as jnp
 from jax import lax
@@ -22,13 +20,8 @@
 CB = FB * PITCH
 VMEM_LIMIT = 16 * 1024 * 1024
 SHIFT = 14.0
-PRECISE = lax.Precision.HIGHEST
 F32 = jnp.float32
 BF16 = jnp.bfloat16
-
-
-def dot(a, b):
-    return lax.dot_general(a, b, (((1,), (0,)), ((), ())), precision=PRECISE, preferred_element_type=F32)
 
 
 def parts(x):
@@ -163,6 +156,14 @@
             f[:, cols] += gg
 
 
+def dot(a, b):
+    m = a.shape[0]
+    a, b = parts(a), parts(b)
+    x = mm(jnp.concatenate(a, 0), b[0])
+    y = mm(jnp.concatenate(a[0:2], 0), b[1])
+    return mm(a[0], b[2]) + y[m:] + x[2 * m :] + y[0:m] + x[m : 2 * m] + x[0:m]
+
+
 def tri(t0, t1, u):
     width = u.shape[1]
     return t0 * u + t1 * pltpu.roll(u, width - 1, 1) + pltpu.roll(t1 * u, 1, 1)
@@ -238,34 +239,49 @@
     split(back, parity, send_e, send_o, 0)
 
 
-def next_kernel(step, copies, rowmat, rowmat_t, t0, t1, diag, before, mom, part, got_e, got_o, vec, mom_out, part_out, send_e, send_o):
-    parity = lax.rem(lax.axis_index("wave"), 2)
+def next_vector(diag, before, part, got_e, got_o):
     prev = before[...]
     d = diag[...]
     image = joined(part, got_e, got_o, 0) + RIDGE * prev
     p = image / d - SHIFT * prev
+    scaled = own(d) * own(p)
+    return p, [lanes_of(scaled * own(prev)), lanes_of(scaled * own(p))]
+
+
+def placed_rows(moments, first, new):
+    row = lax.broadcasted_iota(jnp.int32, moments.shape, 0)
+    for i, value in enumerate(new):
+        moments = jnp.where(row == first + i, value, moments)
+    return moments
+
+
+def third_kernel(rowmat, rowmat_t, t0, t1, diag, before, mom, part, got_e, got_o, vec, mom_out, part_out, send_e, send_o):
+    parity = lax.rem(lax.axis_index("wave"), 2)
+    p, new = next_vector(diag, before, part, got_e, got_o)
     vec[...] = p
-    scaled = own(d) * own(p)
-    u, t, back = apply_rows(p, rowmat, rowmat_t, t0, t1)
-    if copies:
-        part_out[...] = own(back)
-        low, high = back[0:GHOST], back[EXT - GHOST : EXT]
-        send_e[...] = jnp.where(parity == 0, high, low)
-        send_o[...] = jnp.where(parity == 0, low, high)
-    else:
-        part_out[...] = back
-        split(back, parity, send_e, send_o, 0)
-    moments = mom[...]
-    row = lax.broadcasted_iota(jnp.int32, moments.shape, 0)
-    new = [(2 * step - 1, lanes_of(scaled * own(prev))), (2 * step, lanes_of(scaled * own(p)))]
-    if copies:
-        new.append((2 * step + 1, lanes_of(u * t) + RIDGE * lanes_of(own(p) * own(p))))
-    for i, value in new:
-        moments = jnp.where(row == i, value, moments)
-    if copies:
-        mom_out[...] = jnp.broadcast_to(moments[None], mom_out.shape)
-    else:
-        mom_out[...] = moments
+    _, _, back = apply_rows(p, rowmat, rowmat_t, t0, t1)
+    part_out[...] = back
+    split(back, parity, send_e, send_o, 0)
+    mom_out[...] = placed_rows(mom[...], 1, new)
+
+
+def fourth_kernel(rowmat, t0, t1, diag, before, mom, part, got_e, got_o, vec, mom_out, rows_out):
+    p, new = next_vector(diag, before, part, got_e, got_o)
+    vec[...] = p
+    u = dot(rowmat[...], p)
+    t = tri(t0[...], t1[...], u)
+    rows_out[...] = t
+    new.append(lanes_of(u * t) + RIDGE * lanes_of(own(p) * own(p)))
+    mom_out[...] = jnp.broadcast_to(placed_rows(mom[...], 3, new)[None], mom_out.shape)
+
+
+def image_kernel(rowmat_t, rows_in, part_out, send_e, send_o):
+    parity = lax.rem(lax.axis_index("wave"), 2)
+    back = dot(rowmat_t[...], rows_in[...])
+    part_out[...] = own(back)
+    low, high = back[0:GHOST], back[EXT - GHOST : EXT]
+    send_e[...] = jnp.where(parity == 0, high, low)
+    send_o[...] = jnp.where(parity == 0, low, high)
 
 
 def coefficients(mom):
@@ -399,21 +415,35 @@
         compiler_params=small,
         name="second",
     )(rowmat, rowmat_t, t0, t1, start_ext, part, got_e, got_o)
-    vectors = [p0]
-    for step in (1, 2):
-        got_o, got_e = swap(send_o, odd, send_e, even)
-        copies = waves if step == 2 else 0
-        mom_shape = shape(waves, 8, LANES) if copies else shape(8, LANES)
-        vec, mom, part, send_e, send_o = pl.pallas_call(
-            functools.partial(next_kernel, step, copies),
-            in_specs=[vm] * 10,
-            out_specs=[vm] * 5,
-            out_shape=[shape(EXT, width), mom_shape, shape(EXT if step == 1 else slab, width), *[shape(HALF if step == 1 else GHOST, width)] * 2],
-            compiler_params=small,
-        )(rowmat, rowmat_t, t0, t1, diag, vectors[-1], mom, part, got_e, got_o)
-        vectors.append(vec)
     got_o, got_e = swap(send_o, odd, send_e, even)
+    p1, mom, part, send_e, send_o = pl.pallas_call(
+        third_kernel,
+        in_specs=[vm] * 10,
+        out_specs=[vm] * 5,
+        out_shape=[shape(EXT, width), shape(8, LANES), shape(EXT, width), shape(HALF, width), shape(HALF, width)],
+        compiler_params=small,
+        name="third",
+    )(rowmat, rowmat_t, t0, t1, diag, p0, mom, part, got_e, got_o)
+    got_o, got_e = swap(send_o, odd, send_e, even)
+    p2, mom, image_rows = pl.pallas_call(
+        fourth_kernel,
+        in_specs=[vm] * 9,
+        out_specs=[vm] * 3,
+        out_shape=[shape(EXT, width), shape(waves, 8, LANES), shape(rows, width)],
+        compiler_params=small,
+        name="fourth",
+    )(rowmat, t0, t1, diag, p1, mom, part, got_e, got_o)
     moms = lax.all_to_all(mom, "wave", 0, 0)
+    part, send_e, send_o = pl.pallas_call(
+        image_kernel,
+        in_specs=[vm] * 2,
+        out_specs=[vm] * 3,
+        out_shape=[shape(slab, width), shape(GHOST, width), shape(GHOST, width)],
+        compiler_params=small,
+        name="image",
+    )(rowmat_t, image_rows)
+    got_o, got_e = swap(send_o, odd, send_e, even)
+    vectors = (p0, p1, p2)
     return tuple(
         pl.pallas_call(
             last_kernel,

time: 42.9 us -> 42.8 us (level)
    pallas_call x2 -> x3, Pallas kernels: 2.08 us -> 2.31 us  [the longest x1 1.23 us: local(): pl.pallas_call(fourth_kernel, in_specs=[vm] * 9, out_specs=[vm] * 3, out_...]
where the time goes in v4:
time: 42.8 us; the launch traced here: 42.6 us
  starting transfers between devices  17 us (40%)
  waiting for transfers between devices  13.6 us (32%)
  Pallas kernels  10.6 us (25%)
  between operations  1.37 us (3%)
    ppermute x5, waiting for transfers between devices, swap(): got_o = lax.ppermute(send_o, ('tile', 'wave'), odd)  11.4 us
    ppermute x5, starting transfers between devices, swap(): got_o = lax.ppermute(send_o, ('tile', 'wave'), odd)  8.63 us
    all_to_all x1, starting transfers between devices, local(): moms = lax.all_to_all(mom, 'wave', 0, 0)  6.75 us
    pallas_call x1, Pallas kernels, local(): pl.pallas_call(pixel_kernel, in_specs=[sm] + [hb] * 6, out_specs=[vm] * 5...  5.78 us
    all_to_all x1, waiting for transfers between devices, local(): moms = lax.all_to_all(mom, 'wave', 0, 0)  2.24 us
    ppermute x5, starting transfers between devices, swap(): got_e = lax.ppermute(send_e, ('tile', 'wave'), even)  1.58 us
    pallas_call x1, Pallas kernels, local(): pl.pallas_call(fourth_kernel, in_specs=[vm] * 9, out_specs=[vm] * 3, out_...  1.23 us
    pallas_call x1, Pallas kernels, local(): pl.pallas_call(first_kernel, in_specs=[vm] * 8, out_specs=[vm] * 4, out_s...  0.89 us
  transfers between devices with their start and end apart: 11, of which 5 were waited for; matrix products, arithmetic and copies ran while one was open for 0% of the time, Pallas kernels for 14%

profile of v4, /device:TPU:0, one launch (start us, length us, event | category | flops | bytes accessed | tf_op | source)
XLA Modules:
  0.0 42.6 jit_solution(6692416022374686829)
XLA Ops:
  0.6 0.6 %collective-permute-start = (f32[32,500]{1,0:T(8,128)}, f32[32,500]{1,0:T(8,128)S(1)}, u32[]{:S(2)}, u32[]{:S(2)}) collective-permute-start(f32[32,500]{1,0:T(8,128)} %flux.1), channel_id=1, source_target_pairs={{0,1},{1,0},{2,3},{3,2},{4,5},{5,4},{6,7},{7,6},{8,9},{9,8},{10,11... | collective-permute-start | bytes 192008 | tf_op jit(solution)/shard_map/ppermute | solution.py:353
  1.2 2.6 %collective-permute-start.1 = (f32[32,500]{1,0:T(8,128)}, f32[32,500]{1,0:T(8,128)S(1)}, u32[]{:S(2)}, u32[]{:S(2)}) collective-permute-start(f32[32,500]{1,0:T(8,128)} %flux.1), channel_id=1, source_target_pairs={{0,16},{1,2},{2,1},{3,4},{4,3},{5,6},{6,5},{7,8},{8,7},{9,10},{10,... | collective-permute-start | bytes 192008 | tf_op jit(solution)/shard_map/ppermute | solution.py:352
  4.4 0.0 copy-start
  4.4 5.8 %pixels.1 = (f32[128,512]{1,0:T(8,128)S(1)}, f32[128,512]{1,0:T(8,128)S(1)}, f32[128,512]{1,0:T(8,128)S(1)}, f32[128,64]{1,0:T(8,128)S(1)}, f32[64,128]{1,0:T(8,128)S(1)}) custom-call(s32[1]{0:T(128)S(6)} %copy.10.offsets, s32[1,500]{1,0:T(1,128)} %starts.1, f32[12,1,500]{2,1,0:T(1,128)} %bitcast.3, f32[4,16,32]{2,1,0:T(8,128)} %bitcast.2, ...), custom_call_target="tpu_custom_call" | custom-call | tf_op jit(solution)/shard_map/pixels/pallas_call | solution.py:377
  10.2 0.0 collective-permute-done.flux_e
  10.2 0.0 collective-permute-done.1.flux_o
  10.2 0.0 copy-done
  10.3 0.9 %first.1 = (f32[64,512]{1,0:T(8,128)S(1)}, f32[128,512]{1,0:T(8,128)S(1)}, f32[64,512]{1,0:T(8,128)S(1)}, f32[64,512]{1,0:T(8,128)S(1)}) custom-call(f32[32,500]{1,0:T(8,128)S(1)} %copy-done, f32[32,500]{1,0:T(8,128)S(1)} %collective-permute-done.flux_e, f32[32,500]{1,0:T(8,128)S(1)} %collective-permute-done.1.flux_o, f32[128,512]{1,0:T(8,128)S(1)} %get-tuple-element.29.t0, ...), custom_call_target="tpu_custom_call" | custom-call | tf_op jit(solution)/shard_map/first/pallas_call | solution.py:399
  11.1 0.2 collective-permute-start.2
  11.3 1.5 %collective-permute-start.3 = (f32[64,512]{1,0:T(8,128)S(1)}, f32[64,512]{1,0:T(8,128)S(1)}, u32[]{:S(2)}, u32[]{:S(2)}) collective-permute-start(f32[64,512]{1,0:T(8,128)S(1)} %get-tuple-element.36), channel_id=1, source_target_pairs={{0,16},{1,2},{2,1},{3,4},{4,3},{5,6},{6,5},{7,8},{8,7},{9,10},{10,... | collective-permute-start | bytes 393224 | tf_op jit(solution)/shard_map/ppermute | solution.py:352
  12.8 0.0 collective-permute-done.2.got_e
  12.8 3.4 %collective-permute-done.3.got_o = f32[64,512]{1,0:T(8,128)S(1)} collective-permute-done((f32[64,512]{1,0:T(8,128)S(1)}, f32[64,512]{1,0:T(8,128)S(1)}, u32[]{:S(2)}, u32[]{:S(2)}) %collective-permute-start.3) | collective-permute-done | bytes 131104 | tf_op jit(solution)/shard_map/ppermute | solution.py:352
  16.3 0.8 %second.1 = (f32[64,512]{1,0:T(8,128)S(1)}, f32[64,512]{1,0:T(8,128)S(1)}, f32[8,128]{1,0:T(8,128)S(1)}, f32[64,512]{1,0:T(8,128)S(1)}, f32[32,512]{1,0:T(8,128)S(1)}, /*index=5*/f32[32,512]{1,0:T(8,128)S(1)}) custom-call(f32[128,64]{1,0:T(8,128)S(1)} %get-tuple-element.28.rowmat, f32[64,128]{1,0:T(8,128)S(1)} %get-tuple-element.31.rowmat_t, ...), custom_call_target="tpu_custom_call" | custom-call | tf_op jit(solution)/shard_map/second/pallas_call | solution.py:410
  17.1 0.2 collective-permute-start.4
  17.3 1.5 %collective-permute-start.5 = (f32[32,512]{1,0:T(8,128)S(1)}, f32[32,512]{1,0:T(8,128)S(1)}, u32[]{:S(2)}, u32[]{:S(2)}) collective-permute-start(f32[32,512]{1,0:T(8,128)S(1)} %get-tuple-element.42), channel_id=1, source_target_pairs={{0,16},{1,2},{2,1},{3,4},{4,3},{5,6},{6,5},{7,8},{8,7},{9,10},{10,... | collective-permute-start | bytes 196616 | tf_op jit(solution)/shard_map/ppermute | solution.py:352
  18.8 0.0 collective-permute-done.4.got_e
  18.8 2.8 %collective-permute-done.5.got_o = f32[32,512]{1,0:T(8,128)S(1)} collective-permute-done((f32[32,512]{1,0:T(8,128)S(1)}, f32[32,512]{1,0:T(8,128)S(1)}, u32[]{:S(2)}, u32[]{:S(2)}) %collective-permute-start.5) | collective-permute-done | bytes 65568 | tf_op jit(solution)/shard_map/ppermute | solution.py:352
  21.6 0.8 %third.1 = (f32[64,512]{1,0:T(8,128)S(1)}, f32[8,128]{1,0:T(8,128)S(1)}, f32[64,512]{1,0:T(8,128)S(1)}, f32[32,512]{1,0:T(8,128)S(1)}, f32[32,512]{1,0:T(8,128)S(1)}) custom-call(f32[128,64]{1,0:T(8,128)S(1)} %get-tuple-element.28.rowmat, f32[64,128]{1,0:T(8,128)S(1)} %get-tuple-element.31.rowmat_t, f32[128,512]{1,0:T(8,128)S(1)} %get-tuple-element.29.t0, ...), custom_call_target="tpu_custom_call" | custom-call | tf_op jit(solution)/shard_map/third/pallas_call | solution.py:419
  22.4 0.2 collective-permute-start.6
  22.6 1.5 %collective-permute-start.7 = (f32[32,512]{1,0:T(8,128)S(1)}, f32[32,512]{1,0:T(8,128)S(1)}, u32[]{:S(2)}, u32[]{:S(2)}) collective-permute-start(f32[32,512]{1,0:T(8,128)S(1)} %get-tuple-element.47), channel_id=1, source_target_pairs={{0,16},{1,2},{2,1},{3,4},{4,3},{5,6},{6,5},{7,8},{8,7},{9,10},{10,... | collective-permute-start | bytes 196616 | tf_op jit(solution)/shard_map/ppermute | solution.py:352
  24.1 0.0 collective-permute-done.6.got_e
  24.1 2.7 %collective-permute-done.7.got_o = f32[32,512]{1,0:T(8,128)S(1)} collective-permute-done((f32[32,512]{1,0:T(8,128)S(1)}, f32[32,512]{1,0:T(8,128)S(1)}, u32[]{:S(2)}, u32[]{:S(2)}) %collective-permute-start.7) | collective-permute-done | bytes 65568 | tf_op jit(solution)/shard_map/ppermute | solution.py:352
  26.9 1.2 %fourth.1 = (f32[64,512]{1,0:T(8,128)S(1)}, f32[16,8,128]{2,1,0:T(8,128)}, f32[128,512]{1,0:T(8,128)S(1)}) custom-call(f32[128,64]{1,0:T(8,128)S(1)} %get-tuple-element.28.rowmat, f32[128,512]{1,0:T(8,128)S(1)} %get-tuple-element.29.t0, f32[128,512]{1,0:T(8,128)S(1)} %get-tuple-element.30.t1, f32[64,512]{1,0:T(8,128)S(1)} %get-tuple-element.37.diag, ...), custom_call_target="tpu_custom_call" | custom-call | tf_op jit(solution)/shard_map/fourth/pallas_call | solution.py:428
  28.1 6.7 %all-to-all-start = ((f32[16,8,128]{2,1,0:T(8,128)}), f32[16,8,128]{2,1,0:T(8,128)S(1)}, u32[]{:S(2)}, u32[]{:S(2)}) async-start(f32[16,8,128]{2,1,0:T(8,128)} %get-tuple-element.48), calls=%async_computation | async-start | bytes 131072 | tf_op jit(solution)/shard_map/all_to_all | solution.py:436
  34.8 0.3 image.1
  35.1 0.5 %collective-permute-start.8 = (f32[16,512]{1,0:T(8,128)S(1)}, f32[16,512]{1,0:T(8,128)S(1)}, u32[]{:S(2)}, u32[]{:S(2)}) collective-permute-start(f32[16,512]{1,0:T(8,128)S(1)} %get-tuple-element.52), channel_id=1, source_target_pairs={{0,1},{1,0},{2,3},{3,2},{4,5},{5,4},{6,7},{7,6},{8,9},{9,8},{10,11... | collective-permute-start | bytes 98312 | tf_op jit(solution)/shard_map/ppermute | solution.py:353
  35.6 1.5 %collective-permute-start.9 = (f32[16,512]{1,0:T(8,128)S(1)}, f32[16,512]{1,0:T(8,128)S(1)}, u32[]{:S(2)}, u32[]{:S(2)}) collective-permute-start(f32[16,512]{1,0:T(8,128)S(1)} %get-tuple-element.53), channel_id=1, source_target_pairs={{0,16},{1,2},{2,1},{3,4},{4,3},{5,6},{6,5},{7,8},{8,7},{9,10},{10,... | collective-permute-start | bytes 98312 | tf_op jit(solution)/shard_map/ppermute | solution.py:352
  37.1 0.0 collective-permute-done.8.got_e
  37.1 2.4 %collective-permute-done.9.got_o = f32[16,512]{1,0:T(8,128)S(1)} collective-permute-done((f32[16,512]{1,0:T(8,128)S(1)}, f32[16,512]{1,0:T(8,128)S(1)}, u32[]{:S(2)}, u32[]{:S(2)}) %collective-permute-start.9) | collective-permute-done | bytes 32800 | tf_op jit(solution)/shard_map/ppermute | solution.py:352
  39.5 2.2 %all-to-all-done.moms = f32[16,8,128]{2,1,0:T(8,128)S(1)} async-done(((f32[16,8,128]{2,1,0:T(8,128)}), f32[16,8,128]{2,1,0:T(8,128)S(1)}, u32[]{:S(2)}, u32[]{:S(2)}) %all-to-all-start) | async-done | bytes 65568 | tf_op jit(solution)/shard_map/all_to_all | solution.py:436
  41.7 0.8 %last.1 = (f32[32,500]{1,0:T(8,128)}, f32[32,500]{1,0:T(8,128)}) custom-call(f32[16,8,128]{2,1,0:T(8,128)S(1)} %all-to-all-done.moms, f32[64,512]{1,0:T(8,128)S(1)} %get-tuple-element.37.diag, f32[64,512]{1,0:T(8,128)S(1)} %get-tuple-element.33.start_ext, f32[64,512]{1,0:T(8,128)S(1)} %get-tuple-element.38.before.p0, ...), custom_call_target="tpu_custom_call" | custom-call | tf_op jit(solution)/shard_map/last/pallas_call | solution.py:448
Async XLA Ops:
  0.6 9.6 %collective-permute-start = (f32[32,500]{1,0:T(8,128)}, f32[32,500]{1,0:T(8,128)S(1)}, u32[]{:S(2)}, u32[]{:S(2)}) collective-permute-start(f32[32,500]{1,0:T(8,128)} %flux.1), channel_id=1, source_target_pairs={{0,1},{1,0},{2,3},{3,2},{4,5},{5,4},{6,7},{7,6},{8,9},{9,8},{10,11... | collective-permute-start | bytes 192008 | tf_op jit(solution)/shard_map/ppermute | solution.py:353
  1.2 9.0 %collective-permute-start.1 = (f32[32,500]{1,0:T(8,128)}, f32[32,500]{1,0:T(8,128)S(1)}, u32[]{:S(2)}, u32[]{:S(2)}) collective-permute-start(f32[32,500]{1,0:T(8,128)} %flux.1), channel_id=1, source_target_pairs={{0,16},{1,2},{2,1},{3,4},{4,3},{5,6},{6,5},{7,8},{8,7},{9,10},{10,... | collective-permute-start | bytes 192008 | tf_op jit(solution)/shard_map/ppermute | solution.py:352
  4.4 5.8 %copy-start = (f32[32,500]{1,0:T(8,128)S(1)}, f32[32,500]{1,0:T(8,128)}, u32[]{:S(2)}) copy-start(f32[32,500]{1,0:T(8,128)} %flux.1) | copy-start | bytes 192004
  11.1 1.7 %collective-permute-start.2 = (f32[64,512]{1,0:T(8,128)S(1)}, f32[64,512]{1,0:T(8,128)S(1)}, u32[]{:S(2)}, u32[]{:S(2)}) collective-permute-start(f32[64,512]{1,0:T(8,128)S(1)} %get-tuple-element.35), channel_id=1, source_target_pairs={{0,1},{1,0},{2,3},{3,2},{4,5},{5,4},{6,7},{7,6},{8,9},{9,8},{10,11... | collective-permute-start | bytes 393224 | tf_op jit(solution)/shard_map/ppermute | solution.py:353
  11.3 5.0 %collective-permute-start.3 = (f32[64,512]{1,0:T(8,128)S(1)}, f32[64,512]{1,0:T(8,128)S(1)}, u32[]{:S(2)}, u32[]{:S(2)}) collective-permute-start(f32[64,512]{1,0:T(8,128)S(1)} %get-tuple-element.36), channel_id=1, source_target_pairs={{0,16},{1,2},{2,1},{3,4},{4,3},{5,6},{6,5},{7,8},{8,7},{9,10},{10,... | collective-permute-start | bytes 393224 | tf_op jit(solution)/shard_map/ppermute | solution.py:352
  17.1 1.7 %collective-permute-start.4 = (f32[32,512]{1,0:T(8,128)S(1)}, f32[32,512]{1,0:T(8,128)S(1)}, u32[]{:S(2)}, u32[]{:S(2)}) collective-permute-start(f32[32,512]{1,0:T(8,128)S(1)} %get-tuple-element.41), channel_id=1, source_target_pairs={{0,1},{1,0},{2,3},{3,2},{4,5},{5,4},{6,7},{7,6},{8,9},{9,8},{10,11... | collective-permute-start | bytes 196616 | tf_op jit(solution)/shard_map/ppermute | solution.py:353
  17.3 4.3 %collective-permute-start.5 = (f32[32,512]{1,0:T(8,128)S(1)}, f32[32,512]{1,0:T(8,128)S(1)}, u32[]{:S(2)}, u32[]{:S(2)}) collective-permute-start(f32[32,512]{1,0:T(8,128)S(1)} %get-tuple-element.42), channel_id=1, source_target_pairs={{0,16},{1,2},{2,1},{3,4},{4,3},{5,6},{6,5},{7,8},{8,7},{9,10},{10,... | collective-permute-start | bytes 196616 | tf_op jit(solution)/shard_map/ppermute | solution.py:352
  22.4 1.7 %collective-permute-start.6 = (f32[32,512]{1,0:T(8,128)S(1)}, f32[32,512]{1,0:T(8,128)S(1)}, u32[]{:S(2)}, u32[]{:S(2)}) collective-permute-start(f32[32,512]{1,0:T(8,128)S(1)} %get-tuple-element.46), channel_id=1, source_target_pairs={{0,1},{1,0},{2,3},{3,2},{4,5},{5,4},{6,7},{7,6},{8,9},{9,8},{10,11... | collective-permute-start | bytes 196616 | tf_op jit(solution)/shard_map/ppermute | solution.py:353
  22.6 4.3 %collective-permute-start.7 = (f32[32,512]{1,0:T(8,128)S(1)}, f32[32,512]{1,0:T(8,128)S(1)}, u32[]{:S(2)}, u32[]{:S(2)}) collective-permute-start(f32[32,512]{1,0:T(8,128)S(1)} %get-tuple-element.47), channel_id=1, source_target_pairs={{0,16},{1,2},{2,1},{3,4},{4,3},{5,6},{6,5},{7,8},{8,7},{9,10},{10,... | collective-permute-start | bytes 196616 | tf_op jit(solution)/shard_map/ppermute | solution.py:352
  28.1 13.7 %all-to-all-start = ((f32[16,8,128]{2,1,0:T(8,128)}), f32[16,8,128]{2,1,0:T(8,128)S(1)}, u32[]{:S(2)}, u32[]{:S(2)}) async-start(f32[16,8,128]{2,1,0:T(8,128)} %get-tuple-element.48), calls=%async_computation | async-start | bytes 131072 | tf_op jit(solution)/shard_map/all_to_all | solution.py:436
  35.1 2.0 %collective-permute-start.8 = (f32[16,512]{1,0:T(8,128)S(1)}, f32[16,512]{1,0:T(8,128)S(1)}, u32[]{:S(2)}, u32[]{:S(2)}) collective-permute-start(f32[16,512]{1,0:T(8,128)S(1)} %get-tuple-element.52), channel_id=1, source_target_pairs={{0,1},{1,0},{2,3},{3,2},{4,5},{5,4},{6,7},{7,6},{8,9},{9,8},{10,11... | collective-permute-start | bytes 98312 | tf_op jit(solution)/shard_map/ppermute | solution.py:353
  35.6 3.9 %collective-permute-start.9 = (f32[16,512]{1,0:T(8,128)S(1)}, f32[16,512]{1,0:T(8,128)S(1)}, u32[]{:S(2)}, u32[]{:S(2)}) collective-permute-start(f32[16,512]{1,0:T(8,128)S(1)} %get-tuple-element.53), channel_id=1, source_target_pairs={{0,16},{1,2},{2,1},{3,4},{4,3},{5,6},{6,5},{7,8},{8,7},{9,10},{10,... | collective-permute-start | bytes 98312 | tf_op jit(solution)/shard_map/ppermute | solution.py:352
